TPU v7x, 32 devices: a whole 2x2x4 slice. The times are simulated.
32 devices in a mesh: slab: 8 (over y, x, core), probe: 4 (over z).
Axes of the slice: x: 2, y: 2, z: 4, core: 2. Of those that a mesh axis runs over, the one named last changes fastest.
Arguments:
- probe_fields: bfloat16 [256, 32, 8192], P('probe', 'slab'), may hold values from -6 to 6
- sensor_rows: int32 [4096], replicated, may hold values from 0 to 30, as said below
- sensor_cols: int32 [4096], replicated, may hold values from 0 to 8190
- row_frac: float32 [4096], replicated, may hold values from 0 to 1
- col_frac: float32 [4096], replicated, may hold values from 0 to 1
- sensor_weights: float32 [4096], replicated, may hold values from 0.05 to 1
- owner_order: int32 [4096], replicated, may hold values from 0 to 4095, as said below
Outputs:
- adjoint_sources: bfloat16 [256, 32, 8192], P('probe', 'slab')
- observed: float32 [256, 4096], P('probe', 'slab')
- trace_mean: float32 [], replicated
Inputs may be any that keep to these rules, and one draw needn't show every extreme that they name: `sensor_rows`: rows run from 0 to 30. The sensors whose row lies in one slab of 4 rows number at most 2048, and some slab holds exactly 2048. `owner_order`: A permutation. The 4096 // 8 slots of one owner name at most 256 sensors whose row lies in any one slab, and every owner reaches 256 for some slab.
All inputs are finite; a program needn't handle non-finite values.
Results may differ from a plain program's by a relative error of at most 0.0068.
Values sent between devices are 32-bit elements; how exact they have to be, the bound alone decides.
A program may use at most 64 MiB of HBM per device.

v0:
```python
import functools
import typing

import jax
import jax.numpy as jnp
from jax import lax
from jax.experimental import pallas as pl
from jax.experimental.pallas import tpu as pltpu
from jax.sharding import PartitionSpec as P

LANES = 128
BLOCK = 1024
HALF = 256
FIELDS = 11
F32 = jnp.float32
BF16 = jnp.bfloat16
NT = (((1,), (1,)), ((), ()))
VMEM = pltpu.VMEM
SMEM = pltpu.SMEM
LIMIT = pltpu.CompilerParams(vmem_limit_bytes=60 * 1024 * 1024)


def iota(shape, dim):
    return lax.broadcasted_iota(jnp.int32, shape, dim)


def nt_dot(a, b):
    return lax.dot_general(a, b, NT, preferred_element_type=F32)


def plan_kernel(rows, cap_chunks, blocks, slabs, pair_lines, me_ref, r_ref, c_ref, rf_ref, cf_ref, w_ref, order_ref, plan_ref, marks_ref, places_ref, peak_ref):
    lines = r_ref.shape[0]
    sensors = lines * LANES
    step = min(4, lines)
    me = me_ref[0]
    first = me * rows
    owned = lines * LANES // slabs
    keys_group = 2 * blocks
    keys = 3 * keys_group
    chunks = 3 * cap_chunks

    def wide(x, i):
        return jnp.concatenate([x[i + j : i + j + 1, :] for j in range(step)], axis=1)

    order = order_ref[...]
    slot = iota((lines, LANES), 0) * LANES + iota((lines, LANES), 1)
    found = jnp.zeros((2 * lines, LANES), F32)
    for i in range(0, lines, step):
        target = wide(order, i)
        mine = wide(slot, i)
        here = iota((lines, step * LANES), 0) == (target >> 7)
        stack = jnp.concatenate(
            [jnp.where(here, (mine >> 7).astype(F32), 0.0), jnp.where(here, (mine & 127).astype(F32), 0.0)], axis=0
        ).astype(BF16)
        place = jnp.where(iota((LANES, step * LANES), 0) == (target & 127), 1.0, 0.0).astype(BF16)
        found = found + nt_dot(stack, place)
    slot_hi = found[:lines, :]
    slot_lo = found[lines:, :]

    r = r_ref[...]
    c = c_ref[...]
    rel = r - first + 1
    valid = (rel >= 0) & (rel <= rows)
    group = jnp.where(rel == 0, 0, jnp.where(rel == rows, 2, 1))
    block = c // BLOCK
    inner = c - block * BLOCK
    half = c // HALF
    slot_of = (slot_hi * LANES + slot_lo).astype(jnp.int32)
    owner = slot_of // owned
    home = r // rows
    send_key = jnp.where(home == me, owner, -1)
    recv_key = jnp.where(owner == me, home, -1)
    edge = jnp.where(r - home * rows == rows - 1, home, -1)
    edges = jnp.zeros((slabs, LANES), F32)
    for i in range(lines):
        edges = edges + jnp.where(iota((slabs, LANES), 0) == edge[i : i + 1, :], 1.0, 0.0)
    peak_ref[0] = jnp.max(jnp.sum(edges, axis=1, keepdims=True)).astype(jnp.int32)
    key = group * keys_group + 2 * block + jnp.where(inner == BLOCK - 1, 1, 0)
    key = jnp.where(valid, key, -1)

    count = jnp.zeros((keys, 1), F32)
    for i in range(lines):
        count = count + jnp.sum(jnp.where(iota((keys, LANES), 0) == key[i : i + 1, :], 1.0, 0.0), axis=1, keepdims=True)
    big = jnp.floor(count * (1.0 / 64.0))
    small = count - 64.0 * big
    ka, kb = iota((keys, keys), 0), iota((keys, keys), 1)
    below = jnp.where((kb < ka) & (kb // keys_group == ka // keys_group), 1.0, 0.0).astype(BF16)
    start = 64.0 * jnp.dot(below, jnp.broadcast_to(big, (keys, LANES)).astype(BF16), preferred_element_type=F32)
    start = start + jnp.dot(below, jnp.broadcast_to(small, (keys, LANES)).astype(BF16), preferred_element_type=F32)
    start = start + ((iota((keys, LANES), 0) // keys_group) * (cap_chunks * LANES)).astype(F32)
    wide_keys = marks_ref.shape[1]
    diagonal = iota((keys, wide_keys), 0) == iota((keys, wide_keys), 1)
    marks_ref[...] = jnp.concatenate(
        [jnp.sum(jnp.where(diagonal, x, 0.0), axis=0, keepdims=True) for x in (start[:, :1], start[:, :1] + count)], axis=0
    ).astype(jnp.int32)

    upper = jnp.where(iota((LANES, LANES), 0) < iota((LANES, LANES), 1), 1.0, 0.0).astype(BF16)
    carry = jnp.concatenate([start[:, :1], jnp.zeros((2 * slabs, 1), F32)], axis=0)
    spots, sends, recvs = [], [], []
    for i in range(lines):
        hot = jnp.concatenate(
            [
                jnp.where(iota((keys, LANES), 0) == key[i : i + 1, :], 1.0, 0.0),
                jnp.where(iota((slabs, LANES), 0) == send_key[i : i + 1, :], 1.0, 0.0),
                jnp.where(iota((slabs, LANES), 0) == recv_key[i : i + 1, :], 1.0, 0.0),
            ],
            axis=0,
        )
        before = jnp.dot(hot.astype(BF16), upper, preferred_element_type=F32)
        ranks = hot * (before + carry)
        spots.append(jnp.sum(ranks[:keys], axis=0, keepdims=True))
        sends.append(jnp.sum(ranks[keys : keys + slabs], axis=0, keepdims=True))
        recvs.append(jnp.sum(ranks[keys + slabs :], axis=0, keepdims=True))
        carry = carry + jnp.sum(hot, axis=1, keepdims=True)
    spot = jnp.concatenate(spots, axis=0).astype(jnp.int32)
    spot = jnp.where(valid, spot, -1)
    send = jnp.concatenate(sends, axis=0).astype(jnp.int32)
    recv = jnp.concatenate(recvs, axis=0).astype(jnp.int32)
    send_line = jnp.where(send_key >= 0, owner * pair_lines + (send >> 7), 200)
    recv_line = jnp.where(recv_key >= 0, home * pair_lines + (recv >> 7), -1)

    rf = rf_ref[...]
    cf = cf_ref[...]
    w = w_ref[...]
    rf_top = rf.astype(BF16).astype(F32)
    w_top = w.astype(BF16).astype(F32)
    values = [
        half.astype(F32),
        (c - half * HALF).astype(F32),
        (1.0 - cf).astype(BF16).astype(F32),
        cf.astype(BF16).astype(F32),
        rf_top,
        rf - rf_top,
        w_top,
        w - w_top,
        rel.astype(F32),
        send_line.astype(F32),
        (send & 127).astype(F32),
    ]
    total = jnp.zeros((FIELDS * chunks, LANES), F32)
    for i in range(0, lines, step):
        target = wide(spot, i)
        here = iota((chunks, step * LANES), 0) == (target >> 7)
        stack = jnp.concatenate([jnp.where(here, wide(v, i), 0.0) for v in values], axis=0).astype(BF16)
        place = jnp.where(iota((LANES, step * LANES), 0) == (target & 127), 1.0, 0.0).astype(BF16)
        total = total + nt_dot(stack, place)
    for f in range(FIELDS):
        plan_ref[f] = total[f * chunks : (f + 1) * chunks, :]

    slot_here = slot_of - me * owned
    received = slabs * pair_lines
    found = jnp.zeros((2 * received, LANES), F32)
    for i in range(0, lines, step):
        here = iota((received, step * LANES), 0) == wide(recv_line, i)
        target = wide(slot_here, i)
        stack = jnp.concatenate(
            [jnp.where(here, (target >> 7).astype(F32), 0.0), jnp.where(here, (target & 127).astype(F32), 0.0)], axis=0
        ).astype(BF16)
        place = jnp.where(iota((LANES, step * LANES), 0) == (wide(recv, i) & 127), 1.0, 0.0).astype(BF16)
        found = found + nt_dot(stack, place)
    places_ref[...] = (found[:received] * LANES + found[received:]).astype(jnp.int32)


def column_table(plan_ref, chunk, number):
    line = pl.ds(chunk, 1)
    column = plan_ref[0, line, :] * HALF + plan_ref[1, line, :] - (number * BLOCK).astype(F32)
    low = plan_ref[2, line, :].astype(BF16)
    high = plan_ref[3, line, :].astype(BF16)
    cells = iota((HALF, LANES), 0).astype(F32).astype(BF16)
    pieces = []
    for begin in range(0, BLOCK, HALF):
        near = jnp.clip(column - begin, -2.0, HALF).astype(BF16)
        after = jnp.clip(column - (begin - 1), -2.0, HALF).astype(BF16)
        pieces.append(jnp.where(cells == near, low, jnp.where(cells == after, high, jnp.zeros((), BF16))))
    return jnp.concatenate(pieces, axis=0)


def row_pattern(plan_ref, chunk, rows, depth):
    line = pl.ds(chunk, 1)
    rf = plan_ref[4, line, :] + plan_ref[5, line, :]
    rel = plan_ref[8, line, :].astype(jnp.int32)
    row = iota((depth, LANES), 0) % rows + 1
    return jnp.where(row == rel, 1.0 - rf, jnp.where(row == rel + 1, rf, 0.0))


def group_chunks(marks_ref, group, keys_group, base):
    count = (marks_ref[1, (group + 1) * keys_group - 1] - base + LANES - 1) // LANES
    return jnp.maximum(count, 1)


def chunk_range(marks_ref, group, number, keys_group, cap_chunks):
    at = group * keys_group + 2 * number
    begin = marks_ref[0, jnp.maximum(at - 1, group * keys_group)]
    end = marks_ref[1, at + 1]
    base = group * cap_chunks
    last = base + group_chunks(marks_ref, group, keys_group, base * LANES) - 1
    return jnp.minimum(begin // LANES, last), jnp.where(end > begin, (end + LANES - 1) // LANES, 0)


def forward_kernel(cap_chunks, blocks, field_ref, plan_ref, marks_ref, value_ref, sums, flat):
    probes, rows, _ = field_ref.shape
    depth = probes * rows
    keys_group = 2 * blocks
    number = pl.program_id(0)
    counts = [group_chunks(marks_ref, g, keys_group, g * cap_chunks * LANES) for g in range(3)]

    @pl.when(number == 0)
    def _():
        for g in range(3):

            @pl.loop(0, counts[g])
            def _(k):
                sums[g * cap_chunks + k] = jnp.zeros((depth, LANES), F32)

    block = field_ref[...].reshape(depth, BLOCK)
    flat[...] = block
    ranges = [chunk_range(marks_ref, g, number, keys_group, cap_chunks) for g in range(3)]
    table = jnp.concatenate([column_table(plan_ref, begin, number) for begin, _ in ranges], axis=1)
    part = jnp.dot(block, table, preferred_element_type=F32)
    for g in range(3):
        sums[ranges[g][0]] += part[:, g * LANES : (g + 1) * LANES]
    for g in range(3):

        @pl.loop(ranges[g][0] + 1, ranges[g][1])
        def _(chunk):
            sums[chunk] += jnp.dot(flat[...], column_table(plan_ref, chunk, number), preferred_element_type=F32)

    @pl.when(number == blocks - 1)
    def _():
        fold = jnp.where(iota((probes, depth), 1) // rows == iota((probes, depth), 0), 1.0, 0.0).astype(BF16)
        for g in range(3):

            @pl.loop(0, counts[g])
            def _(k):
                chunk = g * cap_chunks + k
                scaled = (sums[chunk] * row_pattern(plan_ref, chunk, rows, depth)).astype(BF16)
                value_ref[chunk] = jnp.dot(fold, scaled, preferred_element_type=F32)


def swap_kernel(slabs, top, value_ref, above_ref, below_ref, send_sem, recv_sem):
    probe, me = lax.axis_index("probe"), lax.axis_index("slab")
    width = above_ref.shape[0]
    down, up = lax.rem(me + slabs - 1, slabs), lax.rem(me + 1, slabs)
    barrier = pltpu.get_barrier_semaphore()
    for peer in (down, up):
        pl.semaphore_signal(barrier, inc=1, device_id=(peer, probe), device_id_type=pl.DeviceIdType.MESH)
    pl.semaphore_wait(barrier, 2)
    copies = []
    for k, (peer, begin, target) in enumerate(((down, 0, above_ref), (up, top, below_ref))):
        copies.append(
            pltpu.make_async_remote_copy(
                src_ref=value_ref.at[begin : begin + width],
                dst_ref=target,
                send_sem=send_sem.at[k],
                recv_sem=recv_sem.at[k],
                device_id=(peer, probe),
                device_id_type=pl.DeviceIdType.MESH,
            )
        )
    for copy in copies:
        copy.start()
    for copy in copies:
        copy.wait()


def swap(slabs, cap_chunks, width, number, value):
    part = (width, *value.shape[1:])
    any_space = pl.BlockSpec(memory_space=pl.ANY)
    above, below = pl.pallas_call(
        functools.partial(swap_kernel, slabs, 2 * cap_chunks),
        out_shape=(jax.ShapeDtypeStruct(part, F32), jax.ShapeDtypeStruct(part, F32)),
        in_specs=[any_space],
        out_specs=(any_space, any_space),
        scratch_shapes=[pltpu.SemaphoreType.DMA((2,)), pltpu.SemaphoreType.DMA((2,))],
        compiler_params=pltpu.CompilerParams(collective_id=number, has_side_effects=True),
        name="swap",
    )(value)
    return above, below


def merge_kernel(cap_chunks, blocks, value_ref, above_ref, below_ref, plan_ref, marks_ref, spread_ref, packed_ref, squares, parts):
    slabs = packed_ref.shape[0]
    outgoing, probes, _ = parts.shape
    lines = outgoing // slabs
    keys_group = 2 * blocks
    squares[...] = jnp.zeros_like(squares)
    parts[...] = jnp.zeros_like(parts)
    for g in range(3):
        count = group_chunks(marks_ref, g, keys_group, g * cap_chunks * LANES)

        @pl.loop(0, count)
        def _(k):
            chunk = g * cap_chunks + k
            value = value_ref[chunk]
            if g == 0:
                value = value + below_ref[k]
            if g == 2:
                value = value + above_ref[k]
            line = pl.ds(chunk, 1)
            spread = value * (plan_ref[6, line, :] + plan_ref[7, line, :])
            spread_ref[chunk] = spread.astype(BF16)
            if g > 0:
                squares[...] += spread * value
                high = plan_ref[9, line, :].astype(jnp.int32)
                low = plan_ref[10, line, :].astype(jnp.int32)
                place = jnp.where(iota((LANES, LANES), 0) == low, 1.0, 0.0).astype(BF16)
                stack = jnp.concatenate([jnp.where(high == d, value, 0.0) for d in range(outgoing)], axis=0).astype(BF16)
                parts[...] += nt_dot(stack, place).reshape(outgoing, probes, LANES)

    folded = squares[:8, :]
    for d in range(8, probes, 8):
        folded = folded + squares[d : d + 8, :]
    for d in range(slabs):
        for e in range(lines):
            packed_ref[d, e * probes : (e + 1) * probes, :] = parts[d * lines + e]
        packed_ref[d, lines * probes :, :] = folded


def unpack_kernel(groups, scale, packed_ref, places_ref, observed_ref, mean_ref, traces, send_sem, recv_sem):
    slab, me = lax.axis_index("slab"), lax.axis_index("probe")
    slabs = packed_ref.shape[0]
    probes, owned = observed_ref.shape
    lines = places_ref.shape[0] // slabs
    barrier = pltpu.get_barrier_semaphore()
    for k in range(1, groups):
        peer = lax.rem(me + k, groups)
        pl.semaphore_signal(barrier, inc=1, device_id=(slab, peer), device_id_type=pl.DeviceIdType.MESH)
    own = packed_ref[0, lines * probes :, :]
    for d in range(1, slabs):
        own = own + packed_ref[d, lines * probes :, :]
    traces[me] = own
    pl.semaphore_wait(barrier, groups - 1)

    def tile(k, source, peer):
        return pltpu.make_async_remote_copy(
            src_ref=traces.at[me],
            dst_ref=traces.at[source],
            send_sem=send_sem.at[k],
            recv_sem=recv_sem.at[k],
            device_id=(slab, peer),
            device_id_type=pl.DeviceIdType.MESH,
        )

    for k in range(1, groups):
        tile(k, me, lax.rem(me + k, groups)).start()
    total = jnp.zeros((probes, owned), F32)
    for d in range(slabs):
        for e in range(lines):
            at = d * lines + e
            place = jnp.where(iota((owned, LANES), 0) == places_ref[at : at + 1, :], 1.0, 0.0).astype(BF16)
            total = total + nt_dot(packed_ref[d, e * probes : (e + 1) * probes, :].astype(BF16), place)
    observed_ref[...] = total
    for k in range(1, groups):
        source = lax.rem(me + groups - k, groups)
        tile(k, source, source).wait()
    summed = jnp.sum(jnp.sum(traces[...], axis=0), axis=0, keepdims=True)
    mean_ref[...] = jnp.broadcast_to(jnp.sum(summed, axis=1, keepdims=True) * scale, mean_ref.shape)


def adjoint_kernel(cap_chunks, blocks, spread_ref, plan_ref, marks_ref, out_ref, sources, total):
    probes, rows, _ = out_ref.shape
    depth = probes * rows
    keys_group = 2 * blocks
    number = pl.program_id(0)

    @pl.when(number == 0)
    def _():
        raise_rows = jnp.where(iota((depth, probes), 0) // rows == iota((depth, probes), 1), 1.0, 0.0).astype(BF16)
        for g in range(3):
            count = group_chunks(marks_ref, g, keys_group, g * cap_chunks * LANES)

            @pl.loop(0, count)
            def _(k):
                chunk = g * cap_chunks + k
                raised = jnp.dot(raise_rows, spread_ref[chunk], preferred_element_type=F32)
                sources[chunk] = (raised * row_pattern(plan_ref, chunk, rows, depth)).astype(BF16)

    ranges = [chunk_range(marks_ref, g, number, keys_group, cap_chunks) for g in range(3)]
    table = jnp.concatenate([column_table(plan_ref, begin, number) for begin, _ in ranges], axis=1)
    source = jnp.concatenate([sources[begin] for begin, _ in ranges], axis=1)
    total[...] = nt_dot(source, table)
    for g in range(3):

        @pl.loop(ranges[g][0] + 1, ranges[g][1])
        def _(chunk):
            total[...] += nt_dot(sources[chunk], column_table(plan_ref, chunk, number))

    out_ref[...] = total[...].astype(BF16).reshape(probes, rows, BLOCK)


def general(slab_count, probe_groups, probe_fields, sensor_rows, sensor_cols, row_frac, col_frac, sensor_weights, owner_order):
    probes, rows, width = probe_fields.shape
    sensors = sensor_rows.shape[0]
    depth = probes * rows
    lines = sensors // LANES
    blocks = width // BLOCK
    keys = 6 * blocks
    most = min(sensors, 4 * sensors // slab_count)
    cap_chunks = -(-most // (8 * LANES)) * 8
    chunks = 3 * cap_chunks
    pair_lines = -(-most // (slab_count * LANES))
    outgoing = slab_count * pair_lines
    me = jnp.reshape(lax.axis_index("slab"), (1,)).astype(jnp.int32)
    boxed = [x.reshape(lines, LANES) for x in (sensor_rows, sensor_cols, row_frac, col_frac, sensor_weights, owner_order)]
    vmem = pl.BlockSpec(memory_space=VMEM)
    smem = pl.BlockSpec(memory_space=SMEM)
    plan, marks, places, peak = pl.pallas_call(
        functools.partial(plan_kernel, rows, cap_chunks, blocks, slab_count, pair_lines),
        out_shape=(
            jax.ShapeDtypeStruct((FIELDS, chunks, LANES), F32),
            jax.ShapeDtypeStruct((2, -(-keys // LANES) * LANES), jnp.int32),
            jax.ShapeDtypeStruct((outgoing, LANES), jnp.int32),
            jax.ShapeDtypeStruct((1,), jnp.int32),
        ),
        in_specs=[smem] + [vmem] * 6,
        out_specs=(vmem, vmem, vmem, smem),
        compiler_params=LIMIT,
        name="plan",
    )(me, *boxed)
    value = pl.pallas_call(
        functools.partial(forward_kernel, cap_chunks, blocks),
        out_shape=jax.ShapeDtypeStruct((chunks, probes, LANES), F32),
        grid=(blocks,),
        in_specs=[pl.BlockSpec((probes, rows, BLOCK), lambda n: (0, 0, n)), vmem, smem],
        out_specs=vmem,
        scratch_shapes=[VMEM((chunks, depth, LANES), F32), VMEM((depth, BLOCK), BF16)],
        compiler_params=LIMIT,
        name="forward",
    )(probe_fields, plan, marks)
    few = min(cap_chunks, -(-5 * most // (4 * rows * LANES)))

    def merged(above, below):
        return pl.pallas_call(
            functools.partial(merge_kernel, cap_chunks, blocks),
            out_shape=(
                jax.ShapeDtypeStruct((chunks, probes, LANES), BF16),
                jax.ShapeDtypeStruct((slab_count, pair_lines * probes + 8, LANES), F32),
            ),
            in_specs=[vmem, vmem, vmem, vmem, smem],
            out_specs=(vmem, vmem),
            scratch_shapes=[VMEM((probes, LANES), F32), VMEM((outgoing, probes, LANES), F32)],
            compiler_params=LIMIT,
            name="merge",
        )(value, above, below, plan, marks)

    spread, packed = lax.cond(
        peak[0] <= few * LANES,
        lambda: merged(*swap(slab_count, cap_chunks, few, 0, value)),
        lambda: merged(*swap(slab_count, cap_chunks, cap_chunks, 1, value)),
    )
    arrived = lax.all_to_all(packed, "slab", 0, 0, tiled=True)
    adjoint = pl.pallas_call(
        functools.partial(adjoint_kernel, cap_chunks, blocks),
        out_shape=jax.ShapeDtypeStruct((probes, rows, width), BF16),
        grid=(blocks,),
        in_specs=[vmem, vmem, smem],
        out_specs=pl.BlockSpec((probes, rows, BLOCK), lambda n: (0, 0, n)),
        scratch_shapes=[
            VMEM((chunks, depth, LANES), BF16),
            VMEM((depth, BLOCK), F32),
        ],
        compiler_params=LIMIT,
        cost_estimate=pl.CostEstimate(flops=4 * 10**9, bytes_accessed=8 * 10**6, transcendentals=0),
        name="adjoint",
    )(spread, plan, marks)
    observed, mean = pl.pallas_call(
        functools.partial(unpack_kernel, probe_groups, 1.0 / (probes * probe_groups * sensors)),
        out_shape=(
            jax.ShapeDtypeStruct((probes, sensors // slab_count), F32),
            jax.ShapeDtypeStruct((1, LANES), F32),
        ),
        in_specs=[vmem, vmem],
        out_specs=(vmem, vmem),
        scratch_shapes=[
            VMEM((probe_groups, 8, LANES), F32),
            pltpu.SemaphoreType.DMA((probe_groups,)),
            pltpu.SemaphoreType.DMA((probe_groups,)),
        ],
        compiler_params=pltpu.CompilerParams(collective_id=2, has_side_effects=True, vmem_limit_bytes=40 * 1024 * 1024),
        name="unpack",
    )(arrived, places)
    return adjoint, observed, mean[0, 0]


COLS = 256
FAST = 11
ROOM = 28 * 1024 * 1024
SMALL = pltpu.CompilerParams(vmem_limit_bytes=ROOM)


class Geo(typing.NamedTuple):
    rows: int
    probes: int
    slabs: int
    groups: int
    buckets: int
    tiles: int
    lines: int
    owned: int
    quarter: int
    edge_lines: int
    kinds: int


def bf(x):
    return x.astype(BF16)


def cells(rows, width):
    return bf(iota((rows, width), 0).astype(F32))


def match(rows, target):
    grid = cells(min(rows, COLS), target.shape[1])
    pieces = []
    for begin in range(0, rows, COLS):
        size = min(COLS, rows - begin)
        near = bf(jnp.clip(target - begin, -1.0, float(COLS)))
        pieces.append(jnp.where(grid[:size] == near, jnp.ones((), BF16), jnp.zeros((), BF16)))
    return pieces[0] if len(pieces) == 1 else jnp.concatenate(pieces, axis=0)


def observe_kernel(geo, me_ref, r_ref, c_ref, rf_ref, cf_ref, w_ref, order_ref, field_ref, plan_ref, slot_ref, flag_ref, value_ref, tiles, hots, ranks, fold, sem):
    lines, slabs, buckets, owned = geo.lines, geo.slabs, geo.buckets, geo.owned
    loads = 8
    rounds = geo.tiles // loads

    def load(g, j):
        t = g * loads + j
        return pltpu.make_async_copy(field_ref.at[:, t], tiles.at[t], sem.at[g])

    for g in reversed(range(rounds)):
        for j in range(loads):
            load(g, j).start()

    me = me_ref[0]
    step = min(4, lines)
    kinds = geo.kinds

    def wide(x, i):
        return jnp.concatenate([x[i + j : i + j + 1, :] for j in range(step)], axis=1)

    order = order_ref[...]
    slot = iota((lines, LANES), 0) * LANES + iota((lines, LANES), 1)
    order_hi, order_lo = bf((order >> 7).astype(F32)), bf((order & 127).astype(F32))
    order_hi, order_lo = order_hi.astype(F32), order_lo.astype(F32)
    mine_hi, mine_lo = (slot >> 7).astype(F32), (slot & 127).astype(F32)
    found = jnp.zeros((2 * lines, LANES), F32)
    line_cells, lane_cells = cells(lines, step * LANES), cells(LANES, step * LANES)
    zero, one = jnp.zeros((), BF16), jnp.ones((), BF16)
    for i in range(0, lines, step):
        here = line_cells == bf(wide(order_hi, i))
        stack = jnp.concatenate([jnp.where(here, bf(wide(mine_hi, i)), zero), jnp.where(here, bf(wide(mine_lo, i)), zero)], axis=0)
        place = jnp.where(lane_cells == bf(wide(order_lo, i)), one, zero)
        found = found + nt_dot(stack, place)
    slot_of = (found[:lines] * LANES + found[lines:]).astype(jnp.int32)

    r = r_ref[...]
    c = c_ref[...]
    rel = r - me * geo.rows + 1
    valid = (rel >= 0) & (rel <= geo.rows)
    bucket = c // COLS
    owner = slot_of // owned
    home = r // geo.rows
    edge = r - home * geo.rows == geo.rows - 1
    key = jnp.where(valid, bucket, -1)
    send_key = jnp.where(valid, owner, -1)
    first_key = jnp.where(owner == me, home, -1)
    second_key = jnp.where((owner == me) & edge, home + 1, -1)
    edge_key = jnp.where(valid & (rel == 0), 0, jnp.where(valid & (rel == geo.rows), 1, -1))

    def hot_of(i):
        line = slice(i, i + 1)
        recv = iota((slabs, LANES), 0)
        return (
            iota((buckets, LANES), 0) == key[line],
            recv == send_key[line],
            recv == first_key[line],
            recv == second_key[line],
            iota((16, LANES), 0) == edge_key[line],
        )

    for i in range(lines):
        a, b, c1, c2, d = hot_of(i)
        hot = jnp.concatenate([jnp.where(x, 1.0, 0.0) for x in (a, b, c1 | c2, d)], axis=0)
        hots[i * kinds : (i + 1) * kinds, :] = bf(hot)
    upper = iota((LANES, 2 * LANES), 0) < iota((LANES, 2 * LANES), 1)
    upper = bf(jnp.where(upper, 1.0, 0.0))
    before = jnp.dot(hots[...], upper, preferred_element_type=F32)
    carry = jnp.zeros((kinds, LANES), F32)
    for i in range(lines):
        part = before[i * kinds : (i + 1) * kinds]
        rank = part[:, :LANES] + carry
        a, b, c1, c2, d = hot_of(i)
        recv = rank[buckets + slabs : buckets + 2 * slabs]
        picks = (
            (a, rank[:buckets]),
            (b, rank[buckets : buckets + slabs]),
            (c1, recv),
            (c2, recv),
            (d, rank[buckets + 2 * slabs :]),
        )
        for k, (mask, value) in enumerate(picks):
            ranks[k, i : i + 1, :] = jnp.sum(jnp.where(mask, value, 0.0), axis=0, keepdims=True)
        carry = carry + part[:, LANES:]
    capacity = 4.0 * geo.quarter
    row = iota((kinds, LANES), 0)
    limit = jnp.where(row < buckets, float(LANES), jnp.where(row < buckets + 2 * slabs, capacity, float(geo.edge_lines * LANES)))
    over = jnp.sum(jnp.where(carry > limit, 1.0, 0.0), axis=0, keepdims=True)
    flag_ref[...] = jnp.broadcast_to(over, flag_ref.shape)

    spot, send, recv1, recv2, swap = (ranks[k] for k in range(5))
    rf, cf, w = rf_ref[...], cf_ref[...], w_ref[...]
    rf_top, w_top = bf(rf).astype(F32), bf(w).astype(F32)
    send_quarter = jnp.floor((send + 0.5) * (1.0 / geo.quarter))
    swap_line = jnp.floor((swap + 0.5) * (1.0 / LANES))
    values = (
        (c - bucket * COLS).astype(F32),
        bf(1.0 - cf).astype(F32),
        bf(cf).astype(F32),
        rf_top,
        rf - rf_top,
        w_top,
        w - w_top,
        (rel + 1 + 8 * owner).astype(F32),
        send - send_quarter * geo.quarter,
        jnp.minimum(send_quarter, 15.0) + 16.0 * jnp.minimum(jnp.where(edge_key >= 0, swap_line, 0.0), 15.0),
        swap - swap_line * LANES,
    )
    key_value = jnp.where(valid & (spot < LANES), bucket, -1).astype(F32)
    bucket_cells = cells(buckets, step * LANES)
    total = jnp.zeros((FAST * buckets, LANES), F32)
    for i in range(0, lines, step):
        here = bucket_cells == bf(wide(key_value, i))
        stack = jnp.concatenate([jnp.where(here, bf(wide(v, i)), zero) for v in values], axis=0)
        place = jnp.where(lane_cells == bf(jnp.minimum(wide(spot, i), 255.0)), one, zero)
        total = total + nt_dot(stack, place)
    for f in range(FAST):
        plan_ref[f] = total[f * buckets : (f + 1) * buckets, :]

    sent = slabs * geo.quarter

    def position(rank, source, use):
        quarter = jnp.floor((rank + 0.5) * (1.0 / geo.quarter))
        place = quarter * sent + source.astype(F32) * geo.quarter + (rank - quarter * geo.quarter)
        return jnp.where(use, place, 4.0 * sent + 8.0)

    here_slot = slot_of - me * owned
    owned_lines = owned // LANES
    slot_line = jnp.where(owner == me, here_slot >> 7, -1).astype(F32)
    slot_lane = (here_slot & 127).astype(F32)
    fields = []
    for place in (position(recv1, home, owner == me), position(recv2, home + 1, edge)):
        high = jnp.floor(place * (1.0 / 64.0))
        fields += [high, place - 64.0 * high]
    slot_cells = cells(owned_lines, step * LANES)
    pad = -(4 * owned_lines) % 16
    placed = jnp.zeros((4 * owned_lines + pad, LANES), F32)
    for i in range(0, lines, step):
        here = jnp.broadcast_to(wide(slot_line, i), (owned_lines, step * LANES)) == iota((owned_lines, step * LANES), 0).astype(F32)
        stack = [jnp.where(here, wide(v, i), 0.0) for v in fields]
        if pad:
            stack.append(jnp.zeros((pad, step * LANES), F32))
        place = jnp.where(lane_cells == bf(wide(slot_lane, i)), one, zero)
        placed = placed + nt_dot(bf(jnp.concatenate(stack, axis=0)), place)
    for f in range(2):
        at = 2 * f * owned_lines
        slot_ref[f] = placed[at : at + owned_lines] * 64.0 + placed[at + owned_lines : at + 2 * owned_lines]

    depth = geo.rows * geo.probes
    spill = None
    batch = loads // 2
    for g in reversed(range(rounds)):
        for j in range(loads):
            load(g, j).wait()
        group = list(reversed(range(g * batch, (g + 1) * batch)))
        parts = []
        for b in group:
            block = jnp.concatenate([tiles[2 * b].reshape(depth, LANES), tiles[2 * b + 1].reshape(depth, LANES)], axis=1)
            parts.append(jnp.dot(block, bucket_table(plan_ref, b), preferred_element_type=F32))
        for b, part in zip(group, parts):
            value = part[:, :LANES]
            if spill is not None:
                value = value + spill
            spill = part[:, LANES:]
            fold[b] = value
            terms = [fold[b, pl.ds(k, geo.probes, stride=geo.rows), :] * x for k, x in enumerate(row_weights(geo, plan_ref, b))]
            value_ref[b] = functools.reduce(jnp.add, terms)


def bucket_table(plan_ref, b):
    near, low, high = (plan_ref[f, pl.ds(b, 1), :] for f in range(3))
    grid = cells(COLS, LANES)
    zero = jnp.zeros((), BF16)
    main = jnp.where(grid == bf(near), bf(low), jnp.where(grid == bf(near + 1.0), bf(high), zero))
    if isinstance(b, int) and b == 0:
        return jnp.concatenate([main, jnp.zeros((COLS, LANES), BF16)], axis=1)
    before = b - 1 if isinstance(b, int) else jnp.maximum(b - 1, 0)
    last, spill = (plan_ref[f, pl.ds(before, 1), :] for f in (0, 2))
    spill = jnp.where(last == COLS - 1.0, spill, 0.0)
    over = bf(jnp.where(iota((16, LANES), 0) == 0, spill, 0.0))
    over = jnp.concatenate([over, jnp.zeros((COLS - 16, LANES), BF16)], axis=0)
    return jnp.concatenate([main, over], axis=1)


def place_code(plan_ref, b):
    code = plan_ref[7, pl.ds(b, 1), :]
    owner = jnp.floor(code * 0.125)
    return owner, code - 8.0 * owner


def row_weights(geo, plan_ref, b):
    rf = plan_ref[3, pl.ds(b, 1), :] + plan_ref[4, pl.ds(b, 1), :]
    _, rel = place_code(plan_ref, b)
    return [jnp.where(rel == k + 2.0, 1.0 - rf, jnp.where(rel == k + 1.0, rf, 0.0)) for k in range(geo.rows)]


def exchange_kernel(geo, value_ref, plan_ref, flag_ref, adjoint_ref, arrived_ref, total_ref, ok_ref, edges, places, inbox, packed, sources, raised, tiles, sums, swap_send, swap_recv, owner_send, owner_recv, tile_send, tile_recv, sum_send, sum_recv):
    slabs, groups, probes, rows, quarter, buckets = geo.slabs, geo.groups, geo.probes, geo.rows, geo.quarter, geo.buckets
    me, mine = lax.axis_index("slab"), lax.axis_index("probe")
    lines = geo.edge_lines
    zero = jnp.zeros((), BF16)
    batch = 8

    def at(slab, probe):
        return dict(device_id=(slab, probe), device_id_type=pl.DeviceIdType.MESH)

    barrier = pltpu.get_barrier_semaphore()
    for k in range(1, slabs):
        pl.semaphore_signal(barrier, inc=1, **at(lax.rem(me + k, slabs), mine))
    for k in range(1, groups):
        pl.semaphore_signal(barrier, inc=1, **at(me, lax.rem(mine + k, groups)))

    def columns(j):
        return slice(j * LANES, (j + 1) * LANES)

    def edge_fields(b):
        _, rel = place_code(plan_ref, b)
        line = jnp.floor(plan_ref[9, pl.ds(b, 1), :] * (1.0 / 16.0))
        lane = plan_ref[10, pl.ds(b, 1), :]
        return rel, line, lane

    edges[...] = jnp.zeros_like(edges)

    @pl.loop(0, buckets // batch)
    def _(g):
        stacks, spots = [], []
        for j in range(batch):
            b = g * batch + j
            rel, line, lane = edge_fields(b)
            low, high = rel == 1.0, rel == rows + 1.0
            spot = match(2 * LANES, jnp.where(low, lane, jnp.where(high, lane + LANES, -1.0)))
            value = value_ref[b]
            stacks.append(jnp.concatenate([bf(jnp.where(line == float(l), value, 0.0)) for l in range(lines)], axis=0))
            spots.append(spot)
            places[b] = spot
        part = nt_dot(jnp.concatenate(stacks, axis=1), jnp.concatenate(spots, axis=1))
        for side in range(2):
            edges[side] += part[:, columns(side)]

    pl.semaphore_wait(barrier, slabs + groups - 2)
    down, up = lax.rem(me + slabs - 1, slabs), lax.rem(me + 1, slabs)
    swaps = [
        pltpu.make_async_remote_copy(
            src_ref=edges.at[side], dst_ref=inbox.at[1 - side], send_sem=swap_send.at[side], recv_sem=swap_recv.at[side], **at(peer, mine)
        )
        for side, peer in ((0, down), (1, up))
    ]
    for copy in swaps:
        copy.start()

    packed[...] = jnp.zeros_like(packed)

    @pl.loop(0, buckets // batch)
    def _(g):
        hots, quads = [], []
        for j in range(batch):
            b = g * batch + j
            owner, rel = place_code(plan_ref, b)
            code = plan_ref[9, pl.ds(b, 1), :]
            fourth = code - 16.0 * jnp.floor(code * (1.0 / 16.0))
            row = jnp.where(rel > 0.0, owner * quarter + plan_ref[8, pl.ds(b, 1), :], -1.0)
            hots.append(match(slabs * quarter, row))
            value = value_ref[b]
            quads.append(jnp.concatenate([bf(jnp.where(fourth == float(k), value, 0.0)) for k in range(4)], axis=0))
        part = nt_dot(jnp.concatenate(hots, axis=1), jnp.concatenate(quads, axis=1))
        packed[...] += part.reshape(packed.shape)

    def owner_copy(k, source, peer):
        return pltpu.make_async_remote_copy(
            src_ref=packed.at[peer], dst_ref=arrived_ref.at[source], send_sem=owner_send.at[k], recv_sem=owner_recv.at[k], **at(peer, mine)
        )

    for k in range(1, slabs):
        owner_copy(k, me, lax.rem(me + k, slabs)).start()
    arrived_ref[me] = packed[me]

    for copy in swaps:
        copy.wait()
    both = bf(jnp.concatenate([inbox[0], inbox[1]], axis=1))
    sources[0] = jnp.zeros_like(sources[0])
    squares = jnp.zeros((probes, LANES), F32)

    def merge(g, squares):
        spots = jnp.concatenate([places[g * batch + j] for j in range(batch)], axis=1)
        extra = jnp.dot(both, spots, preferred_element_type=F32)
        for j in range(batch):
            b = g * batch + j
            rel, line, _ = edge_fields(b)
            full = value_ref[b]
            for l in range(lines):
                full = full + jnp.where(line == float(l), extra[l * probes : (l + 1) * probes, columns(j)], 0.0)
            spread = full * (plan_ref[5, pl.ds(b, 1), :] + plan_ref[6, pl.ds(b, 1), :])
            squares = squares + jnp.where(rel >= 2.0, spread * full, 0.0)
            for k, weight in enumerate(row_weights(geo, plan_ref, b)):
                raised[j, pl.ds(k, probes, stride=rows), :] = spread * weight
            sources[b + 1] = bf(raised[j])
        return squares

    squares = lax.fori_loop(0, buckets // batch, merge, squares)
    folded = squares[:8]
    for d in range(8, probes, 8):
        folded = folded + squares[d : d + 8]
    tiles[mine] = jnp.concatenate([folded, flag_ref[...]], axis=0)

    def tile_copy(k, source, peer):
        return pltpu.make_async_remote_copy(
            src_ref=tiles.at[mine], dst_ref=tiles.at[source], send_sem=tile_send.at[k], recv_sem=tile_recv.at[k], **at(me, peer)
        )

    for k in range(1, groups):
        tile_copy(k, mine, lax.rem(mine + k, groups)).start()

    @pl.loop(0, buckets // batch)
    def _(g):
        parts = []
        for j in range(batch):
            b = g * batch + j
            source = jnp.concatenate([sources[b + 1], sources[b]], axis=1)
            parts.append(nt_dot(source, bucket_table(plan_ref, b)))
        for j in range(batch):
            for t in range(2):
                adjoint_ref[2 * (g * batch + j) + t] = bf(parts[j][:, columns(t)]).reshape(probes, rows, LANES)

    for k in range(1, groups):
        source = lax.rem(mine + groups - k, groups)
        tile_copy(k, source, source).wait()
    sums[me] = jnp.sum(tiles[...], axis=0)

    def sum_copy(k, source, peer):
        return pltpu.make_async_remote_copy(
            src_ref=sums.at[me], dst_ref=sums.at[source], send_sem=sum_send.at[k], recv_sem=sum_recv.at[k], **at(peer, mine)
        )

    for k in range(1, slabs):
        sum_copy(k, me, lax.rem(me + k, slabs)).start()
    for k in range(1, slabs):
        source = lax.rem(me + slabs - k, slabs)
        owner_copy(k, source, source).wait()
    for k in range(1, slabs):
        source = lax.rem(me + slabs - k, slabs)
        sum_copy(k, source, source).wait()
    total = jnp.sum(sums[...], axis=0)
    total_ref[...] = total
    ok_ref[0] = jnp.max(total[8:]).astype(jnp.int32)


def deliver_kernel(geo, scale, adjoint_ref, arrived_ref, slot_ref, total_ref, out_ref, observed_ref, mean_ref, observed, sem):
    slabs, probes, quarter, owned = geo.slabs, geo.probes, geo.quarter, geo.owned
    loads = 8

    def store(t):
        return pltpu.make_async_copy(adjoint_ref.at[t], out_ref.at[:, t], sem.at[0])

    for t in range(geo.tiles):
        store(t).start()
    sent = slabs * quarter
    arrived = jnp.transpose(arrived_ref[...].reshape(sent, 4 * probes))
    lines = owned // LANES
    spots = [jnp.concatenate([slot_ref[f, l : l + 1, :] for l in range(lines)], axis=1) for f in range(2)]
    total = jnp.zeros((probes, owned), F32)
    for k in range(4):
        hot = match(sent, spots[0] - float(k * sent)) + match(sent, spots[1] - float(k * sent))
        total = total + jnp.dot(bf(arrived[k * probes : (k + 1) * probes]), hot, preferred_element_type=F32)
    observed[...] = total
    pltpu.make_async_copy(observed, observed_ref, sem.at[1]).start()
    summed = jnp.sum(total_ref[:8], axis=0, keepdims=True)
    mean_ref[...] = jnp.broadcast_to(jnp.sum(summed, axis=1, keepdims=True) * scale, mean_ref.shape)
    pltpu.make_async_copy(observed, observed_ref, sem.at[1]).wait()
    for t in range(geo.tiles):
        store(t).wait()


def geometry(slabs, groups, probe_fields, sensors):
    probes, rows, width = probe_fields.shape
    most = min(sensors, 4 * sensors // slabs)
    quarter = -(-(most // slabs + 32) // 32) * 8
    edge_lines = -(-5 * most // (4 * rows * LANES))
    buckets = width // COLS
    return Geo(rows, probes, slabs, groups, buckets, width // LANES, sensors // LANES, sensors // slabs, quarter, edge_lines, buckets + 2 * slabs + 16)


def body(slab_count, probe_groups, probe_fields, *vectors):
    sensors = vectors[0].shape[0]
    geo = geometry(slab_count, probe_groups, probe_fields, sensors)
    probes, rows, width = probe_fields.shape
    depth = probes * rows
    lines, buckets, tiles = geo.lines, geo.buckets, geo.tiles
    me = jnp.reshape(lax.axis_index("slab"), (1,)).astype(jnp.int32)
    boxed = [x.reshape(lines, LANES) for x in vectors]
    field = probe_fields.reshape(probes, rows, tiles, LANES).transpose(0, 2, 1, 3)
    vmem = pl.BlockSpec(memory_space=VMEM)
    smem = pl.BlockSpec(memory_space=SMEM)
    hbm = pl.BlockSpec(memory_space=pltpu.HBM)
    dma = pltpu.SemaphoreType.DMA
    shape = jax.ShapeDtypeStruct
    plan, slots, flags, value = pl.pallas_call(
        functools.partial(observe_kernel, geo),
        out_shape=(
            shape((FAST, buckets, LANES), F32),
            shape((2, geo.owned // LANES, LANES), F32),
            shape((8, LANES), F32),
            shape((buckets, probes, LANES), F32),
        ),
        in_specs=[smem] + [vmem] * 6 + [hbm],
        out_specs=(vmem,) * 4,
        scratch_shapes=[
            VMEM((tiles, probes, rows, LANES), BF16),
            VMEM((lines * geo.kinds, LANES), BF16),
            VMEM((5, lines, LANES), F32),
            VMEM((buckets, depth, LANES), F32),
            dma((tiles // 8,)),
        ],
        compiler_params=SMALL,
        name="observe",
    )(me, *boxed, field)
    edge_rows = geo.edge_lines * probes
    adjoint, arrived, total, flag = pl.pallas_call(
        functools.partial(exchange_kernel, geo),
        out_shape=(
            shape((tiles, probes, rows, LANES), BF16),
            shape((slab_count, geo.quarter, 4 * probes), F32),
            shape((16, LANES), F32),
            shape((1,), jnp.int32),
        ),
        in_specs=[vmem] * 3,
        out_specs=(vmem, vmem, vmem, smem),
        scratch_shapes=[
            VMEM((2, edge_rows, LANES), F32),
            VMEM((buckets, 2 * LANES, LANES), BF16),
            VMEM((2, edge_rows, LANES), F32),
            VMEM((slab_count, geo.quarter, 4 * probes), F32),
            VMEM((buckets + 1, depth, LANES), BF16),
            VMEM((8, depth, LANES), F32),
            VMEM((probe_groups, 16, LANES), F32),
            VMEM((slab_count, 16, LANES), F32),
            dma((2,)),
            dma((2,)),
            dma((slab_count,)),
            dma((slab_count,)),
            dma((probe_groups,)),
            dma((probe_groups,)),
            dma((slab_count,)),
            dma((slab_count,)),
        ],
        compiler_params=pltpu.CompilerParams(collective_id=3, has_side_effects=True, vmem_limit_bytes=ROOM),
        name="exchange",
    )(value, plan, flags)

    def deliver():
        out, observed, mean = pl.pallas_call(
            functools.partial(deliver_kernel, geo, 1.0 / (probes * probe_groups * sensors)),
            out_shape=(
                shape((probes, tiles, rows, LANES), BF16),
                shape((probes, geo.owned), F32),
                shape((1, LANES), F32),
            ),
            in_specs=[vmem] * 4,
            out_specs=(hbm, hbm, vmem),
            scratch_shapes=[VMEM((probes, geo.owned), F32), dma((2,))],
            compiler_params=SMALL,
            name="deliver",
        )(adjoint, arrived, slots, total)
        return out.transpose(0, 2, 1, 3).reshape(probes, rows, width), observed, mean[0, 0]

    return lax.cond(flag[0] == 0, deliver, lambda: general(slab_count, probe_groups, probe_fields, *vectors))


def solution(mesh):
    placed = (P("probe", "slab", None), P(), P(), P(), P(), P(), P())
    return jax.shard_map(
        functools.partial(body, mesh.shape["slab"], mesh.shape["probe"]),
        mesh=mesh,
        in_specs=placed,
        out_specs=(P("probe", "slab", None), P("probe", "slab"), P()),
        check_vma=False,
    )
```

profile of v0, /device:TPU:0, one launch (start us, length us, event | category | flops | bytes accessed | tf_op | source)
XLA Modules:
  0.0 36.5 jit_solution(5821398878795375360)
XLA Ops:
  0.6 0.0 copy-start.6
  0.6 0.0 copy-start.5
  0.7 0.0 copy-start.4
  0.7 0.0 copy-start.3
  0.7 0.0 copy-start.2
  0.7 0.0 copy-start.1
  0.7 7.2 %observe.1 = (f32[11,32,128]{2,1,0:T(8,128)S(1)}, f32[2,4,128]{2,1,0:T(4,128)S(1)}, f32[8,128]{1,0:T(8,128)S(1)}, f32[32,64,128]{2,1,0:T(8,128)S(1)}) custom-call(s32[1]{0:T(128)} %bitcast.11.me_ref, s32[32,128]{1,0:T(8,128)} %bitcast.25, s32[32,128]{1,0:T(8,128)} %bitcast.27, f32[32,128]{1,0:T(8,128)} %bitcast.29, f32[32,128]{1,0:T(8,128)} %bitcast.31, ...), custom_call_target="tpu_custom_call" | custom-call | tf_op jit(solution)/shard_map/observe/pallas_call | solution.py:917
  7.9 21.6 %exchange.1 = (bf16[64,64,4,128]{3,2,1,0:T(4,128)(2,1)}, f32[8,72,256]{2,1,0:T(8,128)S(1)}, f32[16,128]{1,0:T(8,128)S(1)}, s32[1]{0:T(128)}) custom-call(f32[32,64,128]{2,1,0:T(8,128)S(1)} %get-tuple-element.77.value_ref, f32[11,32,128]{2,1,0:T(8,128)S(1)} %get-tuple-element.78.plan_ref, f32[8,128]{1,0:T(8,128)S(1)} %get-tuple-element.79.flag_ref), custom_call_target="tpu_custom_call" | custom-call | tf_op jit(solution)/shard_map/exchange/pallas_call | solution.py:938
  30.2 0.0 copy-done.6
  30.2 0.0 copy-done.5
  30.2 0.0 copy-done.4
  30.2 0.0 copy-done.3
  30.2 0.0 copy-done.2
  30.2 0.0 copy-done.1
  30.2 4.5 %conditional.2 = (f32[64,512]{1,0:T(8,128)S(1)}, bf16[64,4,8192]{2,1,0:T(4,128)(2,1)}, f32[1,128]{1,0:T(1,128)S(1)}) conditional(s32[]{:T(128)} %bitcast.20, (s32[4096]{0:T(1024)S(1)}, s32[4096]{0:T(1024)S(1)}, f32[4096]{0:T(1024)S(1)}, f32[4096]{0:T(1024)S(1)}, f32[4096]{0:T(1024)S(1)}, /*index=5*/s32[4096]{0:T(1024)S(1)}, ...), branch_computations={%region_0.0_spmd, %region_3.0_spmd} | conditional | flops 4000000000 | bytes 9704098 | solution.py:986
  30.2 4.5 %deliver.1 = (bf16[64,64,4,128]{3,2,1,0:T(4,128)(2,1)}, f32[64,512]{1,0:T(8,128)S(1)}, f32[1,128]{1,0:T(1,128)S(1)}) custom-call(bf16[64,64,4,128]{3,2,1,0:T(4,128)(2,1)} %get-tuple-element.59.adjoint_ref, f32[8,72,256]{2,1,0:T(8,128)S(1)} %get-tuple-element.60.arrived_ref, f32[2,4,128]{2,1,0:T(4,128)S(1)} %get-tuple-element.61.slot_ref, ...), custom_call_target="tpu_custom_call" | custom-call | tf_op jit(solution)/shard_map/cond/branch_1_fun/deliver/pallas_call | solution.py:971
  34.7 0.7 %copy.26 = f32[64,512]{1,0:T(8,128)} copy(f32[64,512]{1,0:T(8,128)S(1)} %get-tuple-element.104) | data formatting | bytes 262144
Async XLA Ops:
  0.6 29.5 %copy-start.6 = (s32[4096]{0:T(1024)S(1)}, s32[4096]{0:T(1024)}, u32[]{:S(2)}) copy-start(s32[4096]{0:T(1024)} %param.17) | copy-start | bytes 49156
  0.6 29.5 %copy-start.5 = (f32[4096]{0:T(1024)S(1)}, f32[4096]{0:T(1024)}, u32[]{:S(2)}) copy-start(f32[4096]{0:T(1024)} %param.16) | copy-start | bytes 49156
  0.7 29.5 %copy-start.4 = (f32[4096]{0:T(1024)S(1)}, f32[4096]{0:T(1024)}, u32[]{:S(2)}) copy-start(f32[4096]{0:T(1024)} %param.15) | copy-start | bytes 49156
  0.7 29.5 %copy-start.3 = (f32[4096]{0:T(1024)S(1)}, f32[4096]{0:T(1024)}, u32[]{:S(2)}) copy-start(f32[4096]{0:T(1024)} %param.14) | copy-start | bytes 49156
  0.7 29.5 %copy-start.2 = (s32[4096]{0:T(1024)S(1)}, s32[4096]{0:T(1024)}, u32[]{:S(2)}) copy-start(s32[4096]{0:T(1024)} %param.13) | copy-start | bytes 49156
  0.7 29.5 %copy-start.1 = (s32[4096]{0:T(1024)S(1)}, s32[4096]{0:T(1024)}, u32[]{:S(2)}) copy-start(s32[4096]{0:T(1024)} %param.12) | copy-start | bytes 49156
where the time goes:
time: 36.8 us; the launch traced here: 36.5 us
  Pallas kernels  33.2 us (90%)
  between operations  2.59 us (7%)
  local copies, waits for them, and re-layouts  0.68 us (2%)
    pallas_call x1, Pallas kernels, body(): pl.pallas_call(functools.partial(exchange_kernel, geo), out_shape=(shape(...  21.6 us
    pallas_call x1, Pallas kernels, body(): pl.pallas_call(functools.partial(observe_kernel, geo), out_shape=(shape((...  7.18 us
    pallas_call x1, Pallas kernels, deliver(): pl.pallas_call(functools.partial(deliver_kernel, geo, 1.0 / (probes * pro...  4.46 us

commit v1 on v0

--- a/solution.py
+++ b/solution.py
@@ -715,7 +715,7 @@
     return [jnp.where(rel == k + 2.0, 1.0 - rf, jnp.where(rel == k + 1.0, rf, 0.0)) for k in range(geo.rows)]
 
 
-def exchange_kernel(geo, value_ref, plan_ref, flag_ref, adjoint_ref, arrived_ref, total_ref, ok_ref, edges, places, inbox, packed, sources, raised, tiles, sums, swap_send, swap_recv, owner_send, owner_recv, tile_send, tile_recv, sum_send, sum_recv):
+def exchange_kernel(geo, value_ref, plan_ref, flag_ref, adjoint_ref, arrived_ref, total_ref, ok_ref, edges, places, shares, inbox, packed, sources, raised, tiles, sums, swap_send, swap_recv, owner_send, owner_recv, tile_send, tile_recv, sum_send, sum_recv):
     slabs, groups, probes, rows, quarter, buckets = geo.slabs, geo.groups, geo.probes, geo.rows, geo.quarter, geo.buckets
     me, mine = lax.axis_index("slab"), lax.axis_index("probe")
     lines = geo.edge_lines
@@ -740,7 +740,12 @@
         lane = plan_ref[10, pl.ds(b, 1), :]
         return rel, line, lane
 
+    def weight_of(b):
+        return plan_ref[5, pl.ds(b, 1), :] + plan_ref[6, pl.ds(b, 1), :]
+
     edges[...] = jnp.zeros_like(edges)
+    shares[...] = jnp.zeros_like(shares)
+    share_rows = shares.shape[0]
 
     @pl.loop(0, buckets // batch)
     def _(g):
@@ -751,12 +756,14 @@
             low, high = rel == 1.0, rel == rows + 1.0
             spot = match(2 * LANES, jnp.where(low, lane, jnp.where(high, lane + LANES, -1.0)))
             value = value_ref[b]
-            stacks.append(jnp.concatenate([bf(jnp.where(line == float(l), value, 0.0)) for l in range(lines)], axis=0))
+            share = jnp.where((iota((share_rows, LANES), 0).astype(F32) == line) & high, weight_of(b), 0.0)
+            stacks.append(jnp.concatenate([bf(jnp.where(line == float(l), value, 0.0)) for l in range(lines)] + [bf(share)], axis=0))
             spots.append(spot)
             places[b] = spot
         part = nt_dot(jnp.concatenate(stacks, axis=1), jnp.concatenate(spots, axis=1))
         for side in range(2):
-            edges[side] += part[:, columns(side)]
+            edges[side] += part[: lines * probes, columns(side)]
+        shares[...] += part[lines * probes :, columns(1)]
 
     pl.semaphore_wait(barrier, slabs + groups - 2)
     down, up = lax.rem(me + slabs - 1, slabs), lax.rem(me + 1, slabs)
@@ -771,8 +778,7 @@
 
     packed[...] = jnp.zeros_like(packed)
 
-    @pl.loop(0, buckets // batch)
-    def _(g):
+    def pack(g, squares):
         hots, quads = [], []
         for j in range(batch):
             b = g * batch + j
@@ -782,9 +788,13 @@
             row = jnp.where(rel > 0.0, owner * quarter + plan_ref[8, pl.ds(b, 1), :], -1.0)
             hots.append(match(slabs * quarter, row))
             value = value_ref[b]
+            squares = squares + value * value * weight_of(b)
             quads.append(jnp.concatenate([bf(jnp.where(fourth == float(k), value, 0.0)) for k in range(4)], axis=0))
         part = nt_dot(jnp.concatenate(hots, axis=1), jnp.concatenate(quads, axis=1))
         packed[...] += part.reshape(packed.shape)
+        return squares
+
+    squares = lax.fori_loop(0, buckets // batch, pack, jnp.zeros((probes, LANES), F32))
 
     def owner_copy(k, source, peer):
         return pltpu.make_async_remote_copy(
@@ -797,39 +807,39 @@
 
     for copy in swaps:
         copy.wait()
+    for l in range(lines):
+        part = slice(l * probes, (l + 1) * probes)
+        squares = squares + edges[1, part] * inbox[1, part] * (2.0 * shares[l : l + 1])
+    folded = squares[:8]
+    for d in range(8, probes, 8):
+        folded = folded + squares[d : d + 8]
+    tiles[mine] = jnp.concatenate([folded, flag_ref[...]], axis=0)
+
+    def tile_copy(k, source, peer):
+        return pltpu.make_async_remote_copy(
+            src_ref=tiles.at[mine], dst_ref=tiles.at[source], send_sem=tile_send.at[k], recv_sem=tile_recv.at[k], **at(me, peer)
+        )
+
+    for k in range(1, groups):
+        tile_copy(k, mine, lax.rem(mine + k, groups)).start()
+
     both = bf(jnp.concatenate([inbox[0], inbox[1]], axis=1))
     sources[0] = jnp.zeros_like(sources[0])
-    squares = jnp.zeros((probes, LANES), F32)
-
-    def merge(g, squares):
+
+    @pl.loop(0, buckets // batch)
+    def _(g):
         spots = jnp.concatenate([places[g * batch + j] for j in range(batch)], axis=1)
         extra = jnp.dot(both, spots, preferred_element_type=F32)
         for j in range(batch):
             b = g * batch + j
-            rel, line, _ = edge_fields(b)
+            _, line, _ = edge_fields(b)
             full = value_ref[b]
             for l in range(lines):
                 full = full + jnp.where(line == float(l), extra[l * probes : (l + 1) * probes, columns(j)], 0.0)
-            spread = full * (plan_ref[5, pl.ds(b, 1), :] + plan_ref[6, pl.ds(b, 1), :])
-            squares = squares + jnp.where(rel >= 2.0, spread * full, 0.0)
+            spread = full * weight_of(b)
             for k, weight in enumerate(row_weights(geo, plan_ref, b)):
                 raised[j, pl.ds(k, probes, stride=rows), :] = spread * weight
             sources[b + 1] = bf(raised[j])
-        return squares
-
-    squares = lax.fori_loop(0, buckets // batch, merge, squares)
-    folded = squares[:8]
-    for d in range(8, probes, 8):
-        folded = folded + squares[d : d + 8]
-    tiles[mine] = jnp.concatenate([folded, flag_ref[...]], axis=0)
-
-    def tile_copy(k, source, peer):
-        return pltpu.make_async_remote_copy(
-            src_ref=tiles.at[mine], dst_ref=tiles.at[source], send_sem=tile_send.at[k], recv_sem=tile_recv.at[k], **at(me, peer)
-        )
-
-    for k in range(1, groups):
-        tile_copy(k, mine, lax.rem(mine + k, groups)).start()
 
     @pl.loop(0, buckets // batch)
     def _(g):
@@ -948,6 +958,7 @@
         scratch_shapes=[
             VMEM((2, edge_rows, LANES), F32),
             VMEM((buckets, 2 * LANES, LANES), BF16),
+            VMEM((-(-geo.edge_lines // 16) * 16, LANES), F32),
             VMEM((2, edge_rows, LANES), F32),
             VMEM((slab_count, geo.quarter, 4 * probes), F32),
             VMEM((buckets + 1, depth, LANES), BF16),
@@ -967,23 +978,27 @@
         name="exchange",
     )(value, plan, flags)
 
-    def deliver():
-        out, observed, mean = pl.pallas_call(
-            functools.partial(deliver_kernel, geo, 1.0 / (probes * probe_groups * sensors)),
-            out_shape=(
-                shape((probes, tiles, rows, LANES), BF16),
-                shape((probes, geo.owned), F32),
-                shape((1, LANES), F32),
-            ),
-            in_specs=[vmem] * 4,
-            out_specs=(hbm, hbm, vmem),
-            scratch_shapes=[VMEM((probes, geo.owned), F32), dma((2,))],
-            compiler_params=SMALL,
-            name="deliver",
-        )(adjoint, arrived, slots, total)
-        return out.transpose(0, 2, 1, 3).reshape(probes, rows, width), observed, mean[0, 0]
-
-    return lax.cond(flag[0] == 0, deliver, lambda: general(slab_count, probe_groups, probe_fields, *vectors))
+    out, observed, mean = pl.pallas_call(
+        functools.partial(deliver_kernel, geo, 1.0 / (probes * probe_groups * sensors)),
+        out_shape=(
+            shape((probes, tiles, rows, LANES), BF16),
+            shape((probes, geo.owned), F32),
+            shape((1, LANES), F32),
+        ),
+        in_specs=[vmem] * 4,
+        out_specs=(hbm, hbm, vmem),
+        scratch_shapes=[VMEM((probes, geo.owned), F32), dma((2,))],
+        compiler_params=SMALL,
+        name="deliver",
+    )(adjoint, arrived, slots, total)
+    out = out.transpose(0, 2, 1, 3).reshape(probes, rows, width)
+
+    def again(state):
+        out, observed, mean = general(slab_count, probe_groups, probe_fields, *vectors)
+        return out, jnp.where(state[3] > 0, observed, state[1]), mean, state[3] * 0
+
+    state = lax.while_loop(lambda state: state[3] != 0, again, (out, observed, mean[0, 0], flag[0]))
+    return state[:3]
 
 
 def solution(mesh):

time: 36.8 us -> 33.2 us (0.902)
  Pallas kernels: 33.2 us -> 29.5 us
  loops' own time: 0.02 us -> 0.82 us
  local copies, waits for them, and re-layouts: 0.68 us -> 0.12 us
    pallas_call x1, Pallas kernels: 21.6 us -> 19.5 us  [body(): pl.pallas_call(functools.partial(exchange_kernel, geo), out_shape=(shape(...]
    pallas_call x1, Pallas kernels: 4.46 us -> 2.88 us  [body(): pl.pallas_call(functools.partial(deliver_kernel, geo, 1.0 / (probes * pro...]
    another operation x1, loops' own time: 0.02 us -> 0.82 us  [body(): lax.while_loop(lambda state: state[3] != 0, again, (out, observed, mean[0...]
    unnamed x13 -> x14, local copies, waits for them, and re-layouts: 0.68 us -> 0.12 us
where the time goes in v1:
time: 33.2 us; the launch traced here: 32.9 us
  Pallas kernels  29.5 us (89%)
  between operations  2.46 us (7%)
  loops' own time  0.82 us (2%)
    pallas_call x1, Pallas kernels, body(): pl.pallas_call(functools.partial(exchange_kernel, geo), out_shape=(shape(...  19.5 us
    pallas_call x1, Pallas kernels, body(): pl.pallas_call(functools.partial(observe_kernel, geo), out_shape=(shape((...  7.19 us
    pallas_call x1, Pallas kernels, body(): pl.pallas_call(functools.partial(deliver_kernel, geo, 1.0 / (probes * pro...  2.88 us
    another operation x1, loops' own time, body(): lax.while_loop(lambda state: state[3] != 0, again, (out, observed, mean[0...  0.82 us

profile of v1, /device:TPU:0, one launch (start us, length us, event | category | flops | bytes accessed | tf_op | source)
XLA Modules:
  0.0 32.9 jit_solution(14686261473684182582)
XLA Ops:
  0.6 0.0 copy-start.2
  0.6 0.0 copy-start.3
  0.7 0.0 copy-start.4
  0.7 0.0 copy-start.5
  0.7 0.0 copy-start.6
  0.7 0.0 copy-start.7
  0.7 7.2 %observe.1 = (f32[11,32,128]{2,1,0:T(8,128)S(1)}, f32[2,4,128]{2,1,0:T(4,128)S(1)}, f32[8,128]{1,0:T(8,128)S(1)}, f32[32,64,128]{2,1,0:T(8,128)S(1)}) custom-call(s32[1]{0:T(128)} %bitcast.9.me_ref, s32[32,128]{1,0:T(8,128)} %bitcast.27, s32[32,128]{1,0:T(8,128)} %bitcast.29, f32[32,128]{1,0:T(8,128)} %bitcast.31, f32[32,128]{1,0:T(8,128)} %bitcast.33, ...), custom_call_target="tpu_custom_call" | custom-call | tf_op jit(solution)/shard_map/observe/pallas_call | solution.py:927
  7.9 19.5 %exchange.1 = (bf16[64,64,4,128]{3,2,1,0:T(4,128)(2,1)S(1)}, f32[8,72,256]{2,1,0:T(8,128)S(1)}, f32[16,128]{1,0:T(8,128)S(1)}, s32[1]{0:T(128)}) custom-call(f32[32,64,128]{2,1,0:T(8,128)S(1)} %get-tuple-element.101.value_ref, f32[11,32,128]{2,1,0:T(8,128)S(1)} %get-tuple-element.102.plan_ref, f32[8,128]{1,0:T(8,128)S(1)} %get-tuple-element.103.flag_ref), custom_call_target="tpu_custom_call" | custom-call | tf_op jit(solution)/shard_map/exchange/pallas_call | solution.py:948
  27.4 2.9 %deliver.1 = (bf16[64,64,4,128]{3,2,1,0:T(4,128)(2,1)}, f32[64,512]{1,0:T(8,128)S(1)}, f32[1,128]{1,0:T(1,128)}) custom-call(bf16[64,64,4,128]{3,2,1,0:T(4,128)(2,1)S(1)} %get-tuple-element.104.adjoint_ref, f32[8,72,256]{2,1,0:T(8,128)S(1)} %get-tuple-element.105.arrived_ref, f32[2,4,128]{2,1,0:T(4,128)S(1)} %get-tuple-element.106.slot_ref, ...), custom_call_target="tpu_custom_call" | custom-call | tf_op jit(solution)/shard_map/deliver/pallas_call | solution.py:981
  30.3 0.0 copy-done.2
  30.3 0.0 copy-done.3
  30.3 0.0 copy-done.4
  30.3 0.0 copy-done.5
  30.3 0.0 copy-done.6
  30.3 0.0 copy-done.7
  30.3 0.8 %while.13 = (bf16[64,4,8192]{2,1,0:T(4,128)(2,1)}, f32[64,512]{1,0:T(8,128)S(1)}, f32[]{:T(128)}, s32[]{:T(128)}, s32[4096]{0:T(1024)S(1)}, /*index=5*/s32[4096]...) while((bf16[64,4,8192]{2,1,0:T(4,128)(2,1)}, ...), condition=%region_3.4_spmd, body=%region_0.3_spmd | while | flops 4000032768 | bytes 10097413 | solution.py:1000
  31.1 0.0 copy-start.1
  31.7 0.1 copy-done.1
Async XLA Ops:
  0.6 29.6 %copy-start.2 = (s32[4096]{0:T(1024)S(1)}, s32[4096]{0:T(1024)}, u32[]{:S(2)}) copy-start(s32[4096]{0:T(1024)} %param.12) | copy-start | bytes 49156
  0.6 29.6 %copy-start.3 = (s32[4096]{0:T(1024)S(1)}, s32[4096]{0:T(1024)}, u32[]{:S(2)}) copy-start(s32[4096]{0:T(1024)} %param.13) | copy-start | bytes 49156
  0.7 29.6 %copy-start.4 = (f32[4096]{0:T(1024)S(1)}, f32[4096]{0:T(1024)}, u32[]{:S(2)}) copy-start(f32[4096]{0:T(1024)} %param.14) | copy-start | bytes 49156
  0.7 29.6 %copy-start.5 = (f32[4096]{0:T(1024)S(1)}, f32[4096]{0:T(1024)}, u32[]{:S(2)}) copy-start(f32[4096]{0:T(1024)} %param.15) | copy-start | bytes 49156
  0.7 29.6 %copy-start.6 = (f32[4096]{0:T(1024)S(1)}, f32[4096]{0:T(1024)}, u32[]{:S(2)}) copy-start(f32[4096]{0:T(1024)} %param.16) | copy-start | bytes 49156
  0.7 29.6 %copy-start.7 = (s32[4096]{0:T(1024)S(1)}, s32[4096]{0:T(1024)}, u32[]{:S(2)}) copy-start(s32[4096]{0:T(1024)} %param.17) | copy-start | bytes 49156
  31.1 0.7 %copy-start.1 = (f32[64,512]{1,0:T(8,128)}, f32[64,512]{1,0:T(8,128)S(1)}, u32[]{:S(2)}) copy-start(f32[64,512]{1,0:T(8,128)S(1)} %get-tuple-element.189) | copy-start | bytes 393220

commit v2 on v1

--- a/solution.py
+++ b/solution.py
@@ -484,7 +484,7 @@
 
 COLS = 256
 FAST = 11
-ROOM = 28 * 1024 * 1024
+ROOM = 36 * 1024 * 1024
 SMALL = pltpu.CompilerParams(vmem_limit_bytes=ROOM)
 
 
@@ -520,7 +520,7 @@
     return pieces[0] if len(pieces) == 1 else jnp.concatenate(pieces, axis=0)
 
 
-def observe_kernel(geo, me_ref, r_ref, c_ref, rf_ref, cf_ref, w_ref, order_ref, field_ref, plan_ref, slot_ref, flag_ref, value_ref, tiles, hots, ranks, fold, sem):
+def observe(geo, me, r_ref, c_ref, rf_ref, cf_ref, w_ref, order_ref, field_ref, plan_ref, slot_ref, flag_ref, value_ref, tiles, hots, ranks, fold, sem):
     lines, slabs, buckets, owned = geo.lines, geo.slabs, geo.buckets, geo.owned
     loads = 8
     rounds = geo.tiles // loads
@@ -533,7 +533,6 @@
         for j in range(loads):
             load(g, j).start()
 
-    me = me_ref[0]
     step = min(4, lines)
     kinds = geo.kinds
 
@@ -715,7 +714,7 @@
     return [jnp.where(rel == k + 2.0, 1.0 - rf, jnp.where(rel == k + 1.0, rf, 0.0)) for k in range(geo.rows)]
 
 
-def exchange_kernel(geo, value_ref, plan_ref, flag_ref, adjoint_ref, arrived_ref, total_ref, ok_ref, edges, places, shares, inbox, packed, sources, raised, tiles, sums, swap_send, swap_recv, owner_send, owner_recv, tile_send, tile_recv, sum_send, sum_recv):
+def exchange_kernel(geo, r_ref, c_ref, rf_ref, cf_ref, w_ref, order_ref, field_ref, adjoint_ref, arrived_ref, slot_ref, total_ref, ok_ref, plan_ref, flag_ref, value_ref, tiles, hots, ranks, fold, edges, places, shares, inbox, packed, sources, raised, traces, load_sem, swap_send, swap_recv, owner_send, owner_recv, trace_send, trace_recv):
     slabs, groups, probes, rows, quarter, buckets = geo.slabs, geo.groups, geo.probes, geo.rows, geo.quarter, geo.buckets
     me, mine = lax.axis_index("slab"), lax.axis_index("probe")
     lines = geo.edge_lines
@@ -725,11 +724,19 @@
     def at(slab, probe):
         return dict(device_id=(slab, probe), device_id_type=pl.DeviceIdType.MESH)
 
+    everyone = slabs * groups
+    linear = me * groups + mine
+
+    def other(k):
+        return lax.rem(linear + k, everyone)
+
     barrier = pltpu.get_barrier_semaphore()
-    for k in range(1, slabs):
-        pl.semaphore_signal(barrier, inc=1, **at(lax.rem(me + k, slabs), mine))
-    for k in range(1, groups):
-        pl.semaphore_signal(barrier, inc=1, **at(me, lax.rem(mine + k, groups)))
+
+    @pl.loop(1, everyone)
+    def _(k):
+        pl.semaphore_signal(barrier, inc=1, **at(other(k) // groups, other(k) % groups))
+
+    observe(geo, me, r_ref, c_ref, rf_ref, cf_ref, w_ref, order_ref, field_ref, plan_ref, slot_ref, flag_ref, value_ref, tiles, hots, ranks, fold, load_sem)
 
     def columns(j):
         return slice(j * LANES, (j + 1) * LANES)
@@ -765,7 +772,7 @@
             edges[side] += part[: lines * probes, columns(side)]
         shares[...] += part[lines * probes :, columns(1)]
 
-    pl.semaphore_wait(barrier, slabs + groups - 2)
+    pl.semaphore_wait(barrier, everyone - 1)
     down, up = lax.rem(me + slabs - 1, slabs), lax.rem(me + 1, slabs)
     swaps = [
         pltpu.make_async_remote_copy(
@@ -813,15 +820,20 @@
     folded = squares[:8]
     for d in range(8, probes, 8):
         folded = folded + squares[d : d + 8]
-    tiles[mine] = jnp.concatenate([folded, flag_ref[...]], axis=0)
-
-    def tile_copy(k, source, peer):
+    traces[linear] = jnp.concatenate([folded, flag_ref[...]], axis=0)
+
+    def trace_copy(k, source, peer):
         return pltpu.make_async_remote_copy(
-            src_ref=tiles.at[mine], dst_ref=tiles.at[source], send_sem=tile_send.at[k], recv_sem=tile_recv.at[k], **at(me, peer)
+            src_ref=traces.at[linear],
+            dst_ref=traces.at[source],
+            send_sem=trace_send.at[k],
+            recv_sem=trace_recv.at[k],
+            **at(peer // groups, peer % groups),
         )
 
-    for k in range(1, groups):
-        tile_copy(k, mine, lax.rem(mine + k, groups)).start()
+    @pl.loop(1, everyone)
+    def _(k):
+        trace_copy(k, linear, other(k)).start()
 
     both = bf(jnp.concatenate([inbox[0], inbox[1]], axis=1))
     sources[0] = jnp.zeros_like(sources[0])
@@ -852,25 +864,16 @@
             for t in range(2):
                 adjoint_ref[2 * (g * batch + j) + t] = bf(parts[j][:, columns(t)]).reshape(probes, rows, LANES)
 
-    for k in range(1, groups):
-        source = lax.rem(mine + groups - k, groups)
-        tile_copy(k, source, source).wait()
-    sums[me] = jnp.sum(tiles[...], axis=0)
-
-    def sum_copy(k, source, peer):
-        return pltpu.make_async_remote_copy(
-            src_ref=sums.at[me], dst_ref=sums.at[source], send_sem=sum_send.at[k], recv_sem=sum_recv.at[k], **at(peer, mine)
-        )
-
-    for k in range(1, slabs):
-        sum_copy(k, me, lax.rem(me + k, slabs)).start()
     for k in range(1, slabs):
         source = lax.rem(me + slabs - k, slabs)
         owner_copy(k, source, source).wait()
-    for k in range(1, slabs):
-        source = lax.rem(me + slabs - k, slabs)
-        sum_copy(k, source, source).wait()
-    total = jnp.sum(sums[...], axis=0)
+
+    @pl.loop(1, everyone)
+    def _(k):
+        source = lax.rem(linear + everyone - k, everyone)
+        trace_copy(k, source, source).wait()
+
+    total = jnp.sum(traces[...], axis=0)
     total_ref[...] = total
     ok_ref[0] = jnp.max(total[8:]).astype(jnp.int32)
 
@@ -916,7 +919,6 @@
     probes, rows, width = probe_fields.shape
     depth = probes * rows
     lines, buckets, tiles = geo.lines, geo.buckets, geo.tiles
-    me = jnp.reshape(lax.axis_index("slab"), (1,)).astype(jnp.int32)
     boxed = [x.reshape(lines, LANES) for x in vectors]
     field = probe_fields.reshape(probes, rows, tiles, LANES).transpose(0, 2, 1, 3)
     vmem = pl.BlockSpec(memory_space=VMEM)
@@ -924,38 +926,27 @@
     hbm = pl.BlockSpec(memory_space=pltpu.HBM)
     dma = pltpu.SemaphoreType.DMA
     shape = jax.ShapeDtypeStruct
-    plan, slots, flags, value = pl.pallas_call(
-        functools.partial(observe_kernel, geo),
+    edge_rows = geo.edge_lines * probes
+    everyone = slab_count * probe_groups
+    adjoint, arrived, slots, total, flag = pl.pallas_call(
+        functools.partial(exchange_kernel, geo),
         out_shape=(
-            shape((FAST, buckets, LANES), F32),
+            shape((tiles, probes, rows, LANES), BF16),
+            shape((slab_count, geo.quarter, 4 * probes), F32),
             shape((2, geo.owned // LANES, LANES), F32),
-            shape((8, LANES), F32),
-            shape((buckets, probes, LANES), F32),
+            shape((16, LANES), F32),
+            shape((1,), jnp.int32),
         ),
-        in_specs=[smem] + [vmem] * 6 + [hbm],
-        out_specs=(vmem,) * 4,
+        in_specs=[vmem] * 6 + [hbm],
+        out_specs=(vmem, vmem, vmem, vmem, smem),
         scratch_shapes=[
+            VMEM((FAST, buckets, LANES), F32),
+            VMEM((8, LANES), F32),
+            VMEM((buckets, probes, LANES), F32),
             VMEM((tiles, probes, rows, LANES), BF16),
             VMEM((lines * geo.kinds, LANES), BF16),
             VMEM((5, lines, LANES), F32),
             VMEM((buckets, depth, LANES), F32),
-            dma((tiles // 8,)),
-        ],
-        compiler_params=SMALL,
-        name="observe",
-    )(me, *boxed, field)
-    edge_rows = geo.edge_lines * probes
-    adjoint, arrived, total, flag = pl.pallas_call(
-        functools.partial(exchange_kernel, geo),
-        out_shape=(
-            shape((tiles, probes, rows, LANES), BF16),
-            shape((slab_count, geo.quarter, 4 * probes), F32),
-            shape((16, LANES), F32),
-            shape((1,), jnp.int32),
-        ),
-        in_specs=[vmem] * 3,
-        out_specs=(vmem, vmem, vmem, smem),
-        scratch_shapes=[
             VMEM((2, edge_rows, LANES), F32),
             VMEM((buckets, 2 * LANES, LANES), BF16),
             VMEM((-(-geo.edge_lines // 16) * 16, LANES), F32),
@@ -963,21 +954,18 @@
             VMEM((slab_count, geo.quarter, 4 * probes), F32),
             VMEM((buckets + 1, depth, LANES), BF16),
             VMEM((8, depth, LANES), F32),
-            VMEM((probe_groups, 16, LANES), F32),
-            VMEM((slab_count, 16, LANES), F32),
+            VMEM((everyone, 16, LANES), F32),
+            dma((tiles // 8,)),
             dma((2,)),
             dma((2,)),
             dma((slab_count,)),
             dma((slab_count,)),
-            dma((probe_groups,)),
-            dma((probe_groups,)),
-            dma((slab_count,)),
-            dma((slab_count,)),
+            dma((everyone,)),
+            dma((everyone,)),
         ],
         compiler_params=pltpu.CompilerParams(collective_id=3, has_side_effects=True, vmem_limit_bytes=ROOM),
         name="exchange",
-    )(value, plan, flags)
-
+    )(*boxed, field)
     out, observed, mean = pl.pallas_call(
         functools.partial(deliver_kernel, geo, 1.0 / (probes * probe_groups * sensors)),
         out_shape=(

time: 33.2 us -> 34.4 us (1.036)
  Pallas kernels: 29.5 us -> 30.7 us
    pallas_call x1, Pallas kernels: 19.5 us -> 27.8 us  [body(): pl.pallas_call(functools.partial(exchange_kernel, geo), out_shape=(shape(...]
    pallas_call x1 -> x0, Pallas kernels: 7.19 us -> none  [body(): pl.pallas_call(functools.partial(observe_kernel, geo), out_shape=(shape((...]
where the time goes in v2:
time: 34.4 us; the launch traced here: 34.2 us
  Pallas kernels  30.7 us (89%)
  between operations  2.58 us (8%)
  loops' own time  0.8 us (2%)
    pallas_call x1, Pallas kernels, body(): pl.pallas_call(functools.partial(exchange_kernel, geo), out_shape=(shape(...  27.8 us
    pallas_call x1, Pallas kernels, body(): pl.pallas_call(functools.partial(deliver_kernel, geo, 1.0 / (probes * pro...  2.96 us
    another operation x1, loops' own time, body(): lax.while_loop(lambda state: state[3] != 0, again, (out, observed, mean[0...  0.8 us

profile of v2, /device:TPU:0, one launch (start us, length us, event | category | flops | bytes accessed | tf_op | source)
XLA Modules:
  0.0 34.2 jit_solution(8435010645846653353)
XLA Ops:
  0.6 0.0 copy-start.2
  0.6 0.0 copy-start.3
  0.7 0.0 copy-start.4
  0.7 0.0 copy-start.5
  0.7 0.0 copy-start.6
  0.7 0.0 copy-start.7
  0.7 27.8 %exchange.1 = (bf16[64,64,4,128]{3,2,1,0:T(4,128)(2,1)S(1)}, f32[8,72,256]{2,1,0:T(8,128)S(1)}, f32[2,4,128]{2,1,0:T(4,128)S(1)}, f32[16,128]{1,0:T(8,128)S(1)}, s32[1]{0:T(128)}) custom-call(s32[32,128]{1,0:T(8,128)} %bitcast.26, s32[32,128]{1,0:T(8,128)} %bitcast.28, f32[32,128]{1,0:T(8,128)} %bitcast.30, f32[32,128]{1,0:T(8,128)} %bitcast.32, ...), custom_call_target="tpu_custom_call" | custom-call | tf_op jit(solution)/shard_map/exchange/pallas_call | solution.py:931
  28.5 3.0 %deliver.1 = (bf16[64,64,4,128]{3,2,1,0:T(4,128)(2,1)}, f32[64,512]{1,0:T(8,128)S(1)}, f32[1,128]{1,0:T(1,128)}) custom-call(bf16[64,64,4,128]{3,2,1,0:T(4,128)(2,1)S(1)} %get-tuple-element.98.adjoint_ref, f32[8,72,256]{2,1,0:T(8,128)S(1)} %get-tuple-element.99.arrived_ref, f32[2,4,128]{2,1,0:T(4,128)S(1)} %get-tuple-element.100.slot_ref, ...), custom_call_target="tpu_custom_call" | custom-call | tf_op jit(solution)/shard_map/deliver/pallas_call | solution.py:969
  31.4 0.0 copy-done.2
  31.5 0.0 copy-done.3
  31.5 0.0 copy-done.4
  31.5 0.0 copy-done.5
  31.5 0.0 copy-done.6
  31.5 0.0 copy-done.7
  31.5 0.8 %while.13 = (bf16[64,4,8192]{2,1,0:T(4,128)(2,1)}, f32[64,512]{1,0:T(8,128)S(1)}, f32[]{:T(128)}, s32[]{:T(128)}, s32[4096]{0:T(1024)S(1)}, /*index=5*/s32[4096]...) while((bf16[64,4,8192]{2,1,0:T(4,128)(2,1)}, ...), condition=%region_3.4_spmd, body=%region_0.3_spmd | while | flops 4000032768 | bytes 10097413 | solution.py:988
  32.3 0.0 copy-start.1
  33.0 0.0 copy-done.1
Async XLA Ops:
  0.6 30.8 %copy-start.2 = (s32[4096]{0:T(1024)S(1)}, s32[4096]{0:T(1024)}, u32[]{:S(2)}) copy-start(s32[4096]{0:T(1024)} %param.12) | copy-start | bytes 49156
  0.6 30.8 %copy-start.3 = (s32[4096]{0:T(1024)S(1)}, s32[4096]{0:T(1024)}, u32[]{:S(2)}) copy-start(s32[4096]{0:T(1024)} %param.13) | copy-start | bytes 49156
  0.7 30.8 %copy-start.4 = (f32[4096]{0:T(1024)S(1)}, f32[4096]{0:T(1024)}, u32[]{:S(2)}) copy-start(f32[4096]{0:T(1024)} %param.14) | copy-start | bytes 49156
  0.7 30.8 %copy-start.5 = (f32[4096]{0:T(1024)S(1)}, f32[4096]{0:T(1024)}, u32[]{:S(2)}) copy-start(f32[4096]{0:T(1024)} %param.15) | copy-start | bytes 49156
  0.7 30.8 %copy-start.6 = (f32[4096]{0:T(1024)S(1)}, f32[4096]{0:T(1024)}, u32[]{:S(2)}) copy-start(f32[4096]{0:T(1024)} %param.16) | copy-start | bytes 49156
  0.7 30.8 %copy-start.7 = (s32[4096]{0:T(1024)S(1)}, s32[4096]{0:T(1024)}, u32[]{:S(2)}) copy-start(s32[4096]{0:T(1024)} %param.17) | copy-start | bytes 49156
  32.3 0.7 %copy-start.1 = (f32[64,512]{1,0:T(8,128)}, f32[64,512]{1,0:T(8,128)S(1)}, u32[]{:S(2)}) copy-start(f32[64,512]{1,0:T(8,128)S(1)} %get-tuple-element.183) | copy-start | bytes 393220

commit v3 on v2

--- a/solution.py
+++ b/solution.py
@@ -484,6 +484,7 @@
 
 COLS = 256
 FAST = 11
+EARLY = 3
 ROOM = 36 * 1024 * 1024
 SMALL = pltpu.CompilerParams(vmem_limit_bytes=ROOM)
 
@@ -714,7 +715,7 @@
     return [jnp.where(rel == k + 2.0, 1.0 - rf, jnp.where(rel == k + 1.0, rf, 0.0)) for k in range(geo.rows)]
 
 
-def exchange_kernel(geo, r_ref, c_ref, rf_ref, cf_ref, w_ref, order_ref, field_ref, adjoint_ref, arrived_ref, slot_ref, total_ref, ok_ref, plan_ref, flag_ref, value_ref, tiles, hots, ranks, fold, edges, places, shares, inbox, packed, sources, raised, traces, load_sem, swap_send, swap_recv, owner_send, owner_recv, trace_send, trace_recv):
+def exchange_kernel(geo, r_ref, c_ref, rf_ref, cf_ref, w_ref, order_ref, field_ref, adjoint_ref, arrived_ref, slot_ref, total_ref, ok_ref, plan_ref, flag_ref, value_ref, tiles, hots, ranks, fold, edges, places, shares, inbox, packed, sources, raised, traces, sums, load_sem, swap_send, swap_recv, owner_send, owner_recv, trace_send, trace_recv, sum_send, sum_recv):
     slabs, groups, probes, rows, quarter, buckets = geo.slabs, geo.groups, geo.probes, geo.rows, geo.quarter, geo.buckets
     me, mine = lax.axis_index("slab"), lax.axis_index("probe")
     lines = geo.edge_lines
@@ -724,17 +725,11 @@
     def at(slab, probe):
         return dict(device_id=(slab, probe), device_id_type=pl.DeviceIdType.MESH)
 
-    everyone = slabs * groups
-    linear = me * groups + mine
-
-    def other(k):
-        return lax.rem(linear + k, everyone)
-
     barrier = pltpu.get_barrier_semaphore()
-
-    @pl.loop(1, everyone)
-    def _(k):
-        pl.semaphore_signal(barrier, inc=1, **at(other(k) // groups, other(k) % groups))
+    for k in range(1, slabs):
+        pl.semaphore_signal(barrier, inc=1, **at(lax.rem(me + k, slabs), mine))
+    for k in range(1, groups):
+        pl.semaphore_signal(barrier, inc=1, **at(me, lax.rem(mine + k, groups)))
 
     observe(geo, me, r_ref, c_ref, rf_ref, cf_ref, w_ref, order_ref, field_ref, plan_ref, slot_ref, flag_ref, value_ref, tiles, hots, ranks, fold, load_sem)
 
@@ -750,12 +745,10 @@
     def weight_of(b):
         return plan_ref[5, pl.ds(b, 1), :] + plan_ref[6, pl.ds(b, 1), :]
 
-    edges[...] = jnp.zeros_like(edges)
-    shares[...] = jnp.zeros_like(shares)
     share_rows = shares.shape[0]
 
-    @pl.loop(0, buckets // batch)
-    def _(g):
+    found = None
+    for g in range(buckets // batch):
         stacks, spots = [], []
         for j in range(batch):
             b = g * batch + j
@@ -768,11 +761,12 @@
             spots.append(spot)
             places[b] = spot
         part = nt_dot(jnp.concatenate(stacks, axis=1), jnp.concatenate(spots, axis=1))
-        for side in range(2):
-            edges[side] += part[: lines * probes, columns(side)]
-        shares[...] += part[lines * probes :, columns(1)]
-
-    pl.semaphore_wait(barrier, everyone - 1)
+        found = part if found is None else found + part
+    for side in range(2):
+        edges[side] = found[: lines * probes, columns(side)]
+    shares[...] = found[lines * probes :, columns(1)]
+
+    pl.semaphore_wait(barrier, slabs + groups - 2)
     down, up = lax.rem(me + slabs - 1, slabs), lax.rem(me + 1, slabs)
     swaps = [
         pltpu.make_async_remote_copy(
@@ -820,20 +814,15 @@
     folded = squares[:8]
     for d in range(8, probes, 8):
         folded = folded + squares[d : d + 8]
-    traces[linear] = jnp.concatenate([folded, flag_ref[...]], axis=0)
+    traces[mine] = jnp.concatenate([folded, flag_ref[...]], axis=0)
 
     def trace_copy(k, source, peer):
         return pltpu.make_async_remote_copy(
-            src_ref=traces.at[linear],
-            dst_ref=traces.at[source],
-            send_sem=trace_send.at[k],
-            recv_sem=trace_recv.at[k],
-            **at(peer // groups, peer % groups),
+            src_ref=traces.at[mine], dst_ref=traces.at[source], send_sem=trace_send.at[k], recv_sem=trace_recv.at[k], **at(me, peer)
         )
 
-    @pl.loop(1, everyone)
-    def _(k):
-        trace_copy(k, linear, other(k)).start()
+    for k in range(1, groups):
+        trace_copy(k, mine, lax.rem(mine + k, groups)).start()
 
     both = bf(jnp.concatenate([inbox[0], inbox[1]], axis=1))
     sources[0] = jnp.zeros_like(sources[0])
@@ -853,8 +842,7 @@
                 raised[j, pl.ds(k, probes, stride=rows), :] = spread * weight
             sources[b + 1] = bf(raised[j])
 
-    @pl.loop(0, buckets // batch)
-    def _(g):
+    def spread_back(g):
         parts = []
         for j in range(batch):
             b = g * batch + j
@@ -864,16 +852,31 @@
             for t in range(2):
                 adjoint_ref[2 * (g * batch + j) + t] = bf(parts[j][:, columns(t)]).reshape(probes, rows, LANES)
 
+    rounds = buckets // batch
+    early = max(1, rounds * EARLY // 4)
+    pl.loop(0, early)(spread_back)
+    for k in range(1, groups):
+        source = lax.rem(mine + groups - k, groups)
+        trace_copy(k, source, source).wait()
+    sums[me] = jnp.sum(traces[...], axis=0)
+
+    def sum_copy(k, source, peer):
+        return pltpu.make_async_remote_copy(
+            src_ref=sums.at[me], dst_ref=sums.at[source], send_sem=sum_send.at[k], recv_sem=sum_recv.at[k], **at(peer, mine)
+        )
+
+    for k in range(1, slabs):
+        sum_copy(k, me, lax.rem(me + k, slabs)).start()
+
+    if early < rounds:
+        pl.loop(early, rounds)(spread_back)
     for k in range(1, slabs):
         source = lax.rem(me + slabs - k, slabs)
         owner_copy(k, source, source).wait()
-
-    @pl.loop(1, everyone)
-    def _(k):
-        source = lax.rem(linear + everyone - k, everyone)
-        trace_copy(k, source, source).wait()
-
-    total = jnp.sum(traces[...], axis=0)
+    for k in range(1, slabs):
+        source = lax.rem(me + slabs - k, slabs)
+        sum_copy(k, source, source).wait()
+    total = jnp.sum(sums[...], axis=0)
     total_ref[...] = total
     ok_ref[0] = jnp.max(total[8:]).astype(jnp.int32)
 
@@ -927,7 +930,6 @@
     dma = pltpu.SemaphoreType.DMA
     shape = jax.ShapeDtypeStruct
     edge_rows = geo.edge_lines * probes
-    everyone = slab_count * probe_groups
     adjoint, arrived, slots, total, flag = pl.pallas_call(
         functools.partial(exchange_kernel, geo),
         out_shape=(
@@ -954,14 +956,17 @@
             VMEM((slab_count, geo.quarter, 4 * probes), F32),
             VMEM((buckets + 1, depth, LANES), BF16),
             VMEM((8, depth, LANES), F32),
-            VMEM((everyone, 16, LANES), F32),
+            VMEM((probe_groups, 16, LANES), F32),
+            VMEM((slab_count, 16, LANES), F32),
             dma((tiles // 8,)),
             dma((2,)),
             dma((2,)),
             dma((slab_count,)),
             dma((slab_count,)),
-            dma((everyone,)),
-            dma((everyone,)),
+            dma((probe_groups,)),
+            dma((probe_groups,)),
+            dma((slab_count,)),
+            dma((slab_count,)),
         ],
         compiler_params=pltpu.CompilerParams(collective_id=3, has_side_effects=True, vmem_limit_bytes=ROOM),
         name="exchange",

time: 34.4 us -> 31.3 us (0.910)
  Pallas kernels: 30.7 us -> 27.6 us
    pallas_call x1, Pallas kernels: 27.8 us -> 24.7 us  [body(): pl.pallas_call(functools.partial(exchange_kernel, geo), out_shape=(shape(...]
where the time goes in v3:
time: 31.3 us; the launch traced here: 31 us
  Pallas kernels  27.6 us (88%)
  between operations  2.58 us (8%)
  loops' own time  0.8 us (3%)
    pallas_call x1, Pallas kernels, body(): pl.pallas_call(functools.partial(exchange_kernel, geo), out_shape=(shape(...  24.7 us
    pallas_call x1, Pallas kernels, body(): pl.pallas_call(functools.partial(deliver_kernel, geo, 1.0 / (probes * pro...  2.96 us
    another operation x1, loops' own time, body(): lax.while_loop(lambda state: state[3] != 0, again, (out, observed, mean[0...  0.8 us

profile of v3, /device:TPU:0, one launch (start us, length us, event | category | flops | bytes accessed | tf_op | source)
XLA Modules:
  0.0 31.0 jit_solution(9415854962675674107)
XLA Ops:
  0.6 0.0 copy-start.2
  0.6 0.0 copy-start.3
  0.7 0.0 copy-start.4
  0.7 0.0 copy-start.5
  0.7 0.0 copy-start.6
  0.7 0.0 copy-start.7
  0.7 24.7 %exchange.1 = (bf16[64,64,4,128]{3,2,1,0:T(4,128)(2,1)S(1)}, f32[8,72,256]{2,1,0:T(8,128)S(1)}, f32[2,4,128]{2,1,0:T(4,128)S(1)}, f32[16,128]{1,0:T(8,128)S(1)}, s32[1]{0:T(128)}) custom-call(s32[32,128]{1,0:T(8,128)} %bitcast.26, s32[32,128]{1,0:T(8,128)} %bitcast.28, f32[32,128]{1,0:T(8,128)} %bitcast.30, f32[32,128]{1,0:T(8,128)} %bitcast.32, ...), custom_call_target="tpu_custom_call" | custom-call | tf_op jit(solution)/shard_map/exchange/pallas_call | solution.py:933
  25.4 3.0 %deliver.1 = (bf16[64,64,4,128]{3,2,1,0:T(4,128)(2,1)}, f32[64,512]{1,0:T(8,128)S(1)}, f32[1,128]{1,0:T(1,128)}) custom-call(bf16[64,64,4,128]{3,2,1,0:T(4,128)(2,1)S(1)} %get-tuple-element.98.adjoint_ref, f32[8,72,256]{2,1,0:T(8,128)S(1)} %get-tuple-element.99.arrived_ref, f32[2,4,128]{2,1,0:T(4,128)S(1)} %get-tuple-element.100.slot_ref, ...), custom_call_target="tpu_custom_call" | custom-call | tf_op jit(solution)/shard_map/deliver/pallas_call | solution.py:974
  28.3 0.0 copy-done.2
  28.3 0.0 copy-done.3
  28.4 0.0 copy-done.4
  28.4 0.0 copy-done.5
  28.4 0.0 copy-done.6
  28.4 0.0 copy-done.7
  28.4 0.8 %while.13 = (bf16[64,4,8192]{2,1,0:T(4,128)(2,1)}, f32[64,512]{1,0:T(8,128)S(1)}, f32[]{:T(128)}, s32[]{:T(128)}, s32[4096]{0:T(1024)S(1)}, /*index=5*/s32[4096]...) while((bf16[64,4,8192]{2,1,0:T(4,128)(2,1)}, ...), condition=%region_3.4_spmd, body=%region_0.3_spmd | while | flops 4000032768 | bytes 10097413 | solution.py:993
  29.2 0.0 copy-start.1
  29.9 0.0 copy-done.1
Async XLA Ops:
  0.6 27.7 %copy-start.2 = (s32[4096]{0:T(1024)S(1)}, s32[4096]{0:T(1024)}, u32[]{:S(2)}) copy-start(s32[4096]{0:T(1024)} %param.12) | copy-start | bytes 49156
  0.6 27.7 %copy-start.3 = (s32[4096]{0:T(1024)S(1)}, s32[4096]{0:T(1024)}, u32[]{:S(2)}) copy-start(s32[4096]{0:T(1024)} %param.13) | copy-start | bytes 49156
  0.7 27.7 %copy-start.4 = (f32[4096]{0:T(1024)S(1)}, f32[4096]{0:T(1024)}, u32[]{:S(2)}) copy-start(f32[4096]{0:T(1024)} %param.14) | copy-start | bytes 49156
  0.7 27.7 %copy-start.5 = (f32[4096]{0:T(1024)S(1)}, f32[4096]{0:T(1024)}, u32[]{:S(2)}) copy-start(f32[4096]{0:T(1024)} %param.15) | copy-start | bytes 49156
  0.7 27.7 %copy-start.6 = (f32[4096]{0:T(1024)S(1)}, f32[4096]{0:T(1024)}, u32[]{:S(2)}) copy-start(f32[4096]{0:T(1024)} %param.16) | copy-start | bytes 49156
  0.7 27.7 %copy-start.7 = (s32[4096]{0:T(1024)S(1)}, s32[4096]{0:T(1024)}, u32[]{:S(2)}) copy-start(s32[4096]{0:T(1024)} %param.17) | copy-start | bytes 49156
  29.2 0.7 %copy-start.1 = (f32[64,512]{1,0:T(8,128)}, f32[64,512]{1,0:T(8,128)S(1)}, u32[]{:S(2)}) copy-start(f32[64,512]{1,0:T(8,128)S(1)} %get-tuple-element.183) | copy-start | bytes 393220

commit v4 on v3

--- a/solution.py
+++ b/solution.py
@@ -747,6 +747,14 @@
 
     share_rows = shares.shape[0]
 
+    @pl.when(me == 0)
+    def _():
+        inbox[0] = jnp.zeros_like(inbox[0])
+
+    @pl.when(me == slabs - 1)
+    def _():
+        inbox[1] = jnp.zeros_like(inbox[1])
+
     found = None
     for g in range(buckets // batch):
         stacks, spots = [], []
@@ -774,8 +782,9 @@
         )
         for side, peer in ((0, down), (1, up))
     ]
-    for copy in swaps:
-        copy.start()
+    ends = (me > 0, me < slabs - 1)
+    for side, copy in enumerate(swaps):
+        pl.when(ends[side])(copy.start)
 
     packed[...] = jnp.zeros_like(packed)
 
@@ -806,15 +815,16 @@
         owner_copy(k, me, lax.rem(me + k, slabs)).start()
     arrived_ref[me] = packed[me]
 
-    for copy in swaps:
-        copy.wait()
+    for side, copy in enumerate(swaps):
+        pl.when(ends[side])(copy.wait_send)
+        pl.when(ends[1 - side])(copy.wait_recv)
     for l in range(lines):
         part = slice(l * probes, (l + 1) * probes)
         squares = squares + edges[1, part] * inbox[1, part] * (2.0 * shares[l : l + 1])
     folded = squares[:8]
     for d in range(8, probes, 8):
         folded = folded + squares[d : d + 8]
-    traces[mine] = jnp.concatenate([folded, flag_ref[...]], axis=0)
+    traces[mine] = jnp.where(flag_ref[:1] > 0.0, jnp.inf, jnp.sum(folded, axis=0, keepdims=True))
 
     def trace_copy(k, source, peer):
         return pltpu.make_async_remote_copy(
@@ -878,7 +888,7 @@
         sum_copy(k, source, source).wait()
     total = jnp.sum(sums[...], axis=0)
     total_ref[...] = total
-    ok_ref[0] = jnp.max(total[8:]).astype(jnp.int32)
+    ok_ref[0] = jnp.max(jnp.where(total < jnp.inf, 0.0, 1.0)).astype(jnp.int32)
 
 
 def deliver_kernel(geo, scale, adjoint_ref, arrived_ref, slot_ref, total_ref, out_ref, observed_ref, mean_ref, observed, sem):
@@ -900,8 +910,7 @@
         total = total + jnp.dot(bf(arrived[k * probes : (k + 1) * probes]), hot, preferred_element_type=F32)
     observed[...] = total
     pltpu.make_async_copy(observed, observed_ref, sem.at[1]).start()
-    summed = jnp.sum(total_ref[:8], axis=0, keepdims=True)
-    mean_ref[...] = jnp.broadcast_to(jnp.sum(summed, axis=1, keepdims=True) * scale, mean_ref.shape)
+    mean_ref[...] = jnp.broadcast_to(jnp.sum(total_ref[...], axis=1, keepdims=True) * scale, mean_ref.shape)
     pltpu.make_async_copy(observed, observed_ref, sem.at[1]).wait()
     for t in range(geo.tiles):
         store(t).wait()
@@ -936,7 +945,7 @@
             shape((tiles, probes, rows, LANES), BF16),
             shape((slab_count, geo.quarter, 4 * probes), F32),
             shape((2, geo.owned // LANES, LANES), F32),
-            shape((16, LANES), F32),
+            shape((1, LANES), F32),
             shape((1,), jnp.int32),
         ),
         in_specs=[vmem] * 6 + [hbm],
@@ -956,8 +965,8 @@
             VMEM((slab_count, geo.quarter, 4 * probes), F32),
             VMEM((buckets + 1, depth, LANES), BF16),
             VMEM((8, depth, LANES), F32),
-            VMEM((probe_groups, 16, LANES), F32),
-            VMEM((slab_count, 16, LANES), F32),
+            VMEM((probe_groups, 1, LANES), F32),
+            VMEM((slab_count, 1, LANES), F32),
             dma((tiles // 8,)),
             dma((2,)),
             dma((2,)),

time: 31.3 us -> 30.9 us (0.987)
  Pallas kernels: 27.6 us -> 27.2 us
    pallas_call x1, Pallas kernels: 24.7 us -> 24.2 us  [body(): pl.pallas_call(functools.partial(exchange_kernel, geo), out_shape=(shape(...]
where the time goes in v4:
time: 30.9 us; the launch traced here: 30.6 us
  Pallas kernels  27.2 us (88%)
  between operations  2.58 us (8%)
  loops' own time  0.8 us (3%)
    pallas_call x1, Pallas kernels, body(): pl.pallas_call(functools.partial(exchange_kernel, geo), out_shape=(shape(...  24.2 us
    pallas_call x1, Pallas kernels, body(): pl.pallas_call(functools.partial(deliver_kernel, geo, 1.0 / (probes * pro...  2.96 us
    another operation x1, loops' own time, body(): lax.while_loop(lambda state: state[3] != 0, again, (out, observed, mean[0...  0.8 us

profile of v4, /device:TPU:0, one launch (start us, length us, event | category | flops | bytes accessed | tf_op | source)
XLA Modules:
  0.0 30.6 jit_solution(5385548093040551346)
XLA Ops:
  0.6 0.0 copy-start.2
  0.6 0.0 copy-start.3
  0.7 0.0 copy-start.4
  0.7 0.0 copy-start.5
  0.7 0.0 copy-start.6
  0.7 0.0 copy-start.7
  0.7 24.2 %exchange.1 = (bf16[64,64,4,128]{3,2,1,0:T(4,128)(2,1)S(1)}, f32[8,72,256]{2,1,0:T(8,128)S(1)}, f32[2,4,128]{2,1,0:T(4,128)S(1)}, f32[1,128]{1,0:T(1,128)S(1)}, s32[1]{0:T(128)}) custom-call(s32[32,128]{1,0:T(8,128)} %bitcast.26, s32[32,128]{1,0:T(8,128)} %bitcast.28, f32[32,128]{1,0:T(8,128)} %bitcast.30, f32[32,128]{1,0:T(8,128)} %bitcast.32, ...), custom_call_target="tpu_custom_call" | custom-call | tf_op jit(solution)/shard_map/exchange/pallas_call | solution.py:942
  24.9 3.0 %deliver.1 = (bf16[64,64,4,128]{3,2,1,0:T(4,128)(2,1)}, f32[64,512]{1,0:T(8,128)S(1)}, f32[1,128]{1,0:T(1,128)}) custom-call(bf16[64,64,4,128]{3,2,1,0:T(4,128)(2,1)S(1)} %get-tuple-element.98.adjoint_ref, f32[8,72,256]{2,1,0:T(8,128)S(1)} %get-tuple-element.99.arrived_ref, f32[2,4,128]{2,1,0:T(4,128)S(1)} %get-tuple-element.100.slot_ref, ...), custom_call_target="tpu_custom_call" | custom-call | tf_op jit(solution)/shard_map/deliver/pallas_call | solution.py:983
  27.9 0.0 copy-done.2
  27.9 0.0 copy-done.3
  27.9 0.0 copy-done.4
  27.9 0.0 copy-done.5
  27.9 0.0 copy-done.6
  27.9 0.0 copy-done.7
  27.9 0.8 %while.13 = (bf16[64,4,8192]{2,1,0:T(4,128)(2,1)}, f32[64,512]{1,0:T(8,128)S(1)}, f32[]{:T(128)}, s32[]{:T(128)}, s32[4096]{0:T(1024)S(1)}, /*index=5*/s32[4096]...) while((bf16[64,4,8192]{2,1,0:T(4,128)(2,1)}, ...), condition=%region_3.4_spmd, body=%region_0.3_spmd | while | flops 4000032768 | bytes 10097413 | solution.py:1002
  28.7 0.0 copy-start.1
  29.4 0.0 copy-done.1
Async XLA Ops:
  0.6 27.2 %copy-start.2 = (s32[4096]{0:T(1024)S(1)}, s32[4096]{0:T(1024)}, u32[]{:S(2)}) copy-start(s32[4096]{0:T(1024)} %param.12) | copy-start | bytes 49156
  0.6 27.2 %copy-start.3 = (s32[4096]{0:T(1024)S(1)}, s32[4096]{0:T(1024)}, u32[]{:S(2)}) copy-start(s32[4096]{0:T(1024)} %param.13) | copy-start | bytes 49156
  0.7 27.2 %copy-start.4 = (f32[4096]{0:T(1024)S(1)}, f32[4096]{0:T(1024)}, u32[]{:S(2)}) copy-start(f32[4096]{0:T(1024)} %param.14) | copy-start | bytes 49156
  0.7 27.2 %copy-start.5 = (f32[4096]{0:T(1024)S(1)}, f32[4096]{0:T(1024)}, u32[]{:S(2)}) copy-start(f32[4096]{0:T(1024)} %param.15) | copy-start | bytes 49156
  0.7 27.2 %copy-start.6 = (f32[4096]{0:T(1024)S(1)}, f32[4096]{0:T(1024)}, u32[]{:S(2)}) copy-start(f32[4096]{0:T(1024)} %param.16) | copy-start | bytes 49156
  0.7 27.2 %copy-start.7 = (s32[4096]{0:T(1024)S(1)}, s32[4096]{0:T(1024)}, u32[]{:S(2)}) copy-start(s32[4096]{0:T(1024)} %param.17) | copy-start | bytes 49156
  28.7 0.7 %copy-start.1 = (f32[64,512]{1,0:T(8,128)}, f32[64,512]{1,0:T(8,128)S(1)}, u32[]{:S(2)}) copy-start(f32[64,512]{1,0:T(8,128)S(1)} %get-tuple-element.183) | copy-start | bytes 393220

commit v5 on v4

--- a/solution.py
+++ b/solution.py
@@ -811,8 +811,6 @@
             src_ref=packed.at[peer], dst_ref=arrived_ref.at[source], send_sem=owner_send.at[k], recv_sem=owner_recv.at[k], **at(peer, mine)
         )
 
-    for k in range(1, slabs):
-        owner_copy(k, me, lax.rem(me + k, slabs)).start()
     arrived_ref[me] = packed[me]
 
     for side, copy in enumerate(swaps):
@@ -834,6 +832,8 @@
     for k in range(1, groups):
         trace_copy(k, mine, lax.rem(mine + k, groups)).start()
 
+    for k in range(1, slabs):
+        owner_copy(k, me, lax.rem(me + k, slabs)).start()
     both = bf(jnp.concatenate([inbox[0], inbox[1]], axis=1))
     sources[0] = jnp.zeros_like(sources[0])
 

time: 30.9 us -> 30.7 us (level)
  no operation moved by 1% of the time
where the time goes in v5:
time: 30.7 us; the launch traced here: 30.5 us
  Pallas kernels  27 us (88%)
  between operations  2.58 us (8%)
  loops' own time  0.8 us (3%)
    pallas_call x1, Pallas kernels, body(): pl.pallas_call(functools.partial(exchange_kernel, geo), out_shape=(shape(...  24.1 us
    pallas_call x1, Pallas kernels, body(): pl.pallas_call(functools.partial(deliver_kernel, geo, 1.0 / (probes * pro...  2.96 us
    another operation x1, loops' own time, body(): lax.while_loop(lambda state: state[3] != 0, again, (out, observed, mean[0...  0.8 us

profile of v5, /device:TPU:0, one launch (start us, length us, event | category | flops | bytes accessed | tf_op | source)
XLA Modules:
  0.0 30.5 jit_solution(7529613194556417433)
XLA Ops:
  0.6 0.0 copy-start.2
  0.6 0.0 copy-start.3
  0.7 0.0 copy-start.4
  0.7 0.0 copy-start.5
  0.7 0.0 copy-start.6
  0.7 0.0 copy-start.7
  0.7 24.1 %exchange.1 = (bf16[64,64,4,128]{3,2,1,0:T(4,128)(2,1)S(1)}, f32[8,72,256]{2,1,0:T(8,128)S(1)}, f32[2,4,128]{2,1,0:T(4,128)S(1)}, f32[1,128]{1,0:T(1,128)S(1)}, s32[1]{0:T(128)}) custom-call(s32[32,128]{1,0:T(8,128)} %bitcast.26, s32[32,128]{1,0:T(8,128)} %bitcast.28, f32[32,128]{1,0:T(8,128)} %bitcast.30, f32[32,128]{1,0:T(8,128)} %bitcast.32, ...), custom_call_target="tpu_custom_call" | custom-call | tf_op jit(solution)/shard_map/exchange/pallas_call | solution.py:942
  24.8 3.0 %deliver.1 = (bf16[64,64,4,128]{3,2,1,0:T(4,128)(2,1)}, f32[64,512]{1,0:T(8,128)S(1)}, f32[1,128]{1,0:T(1,128)}) custom-call(bf16[64,64,4,128]{3,2,1,0:T(4,128)(2,1)S(1)} %get-tuple-element.98.adjoint_ref, f32[8,72,256]{2,1,0:T(8,128)S(1)} %get-tuple-element.99.arrived_ref, f32[2,4,128]{2,1,0:T(4,128)S(1)} %get-tuple-element.100.slot_ref, ...), custom_call_target="tpu_custom_call" | custom-call | tf_op jit(solution)/shard_map/deliver/pallas_call | solution.py:983
  27.8 0.0 copy-done.2
  27.8 0.0 copy-done.3
  27.8 0.0 copy-done.4
  27.8 0.0 copy-done.5
  27.8 0.0 copy-done.6
  27.8 0.0 copy-done.7
  27.8 0.8 %while.13 = (bf16[64,4,8192]{2,1,0:T(4,128)(2,1)}, f32[64,512]{1,0:T(8,128)S(1)}, f32[]{:T(128)}, s32[]{:T(128)}, s32[4096]{0:T(1024)S(1)}, /*index=5*/s32[4096]...) while((bf16[64,4,8192]{2,1,0:T(4,128)(2,1)}, ...), condition=%region_3.4_spmd, body=%region_0.3_spmd | while | flops 4000032768 | bytes 10097413 | solution.py:1002
  28.6 0.0 copy-start.1
  29.3 0.0 copy-done.1
Async XLA Ops:
  0.6 27.1 %copy-start.2 = (s32[4096]{0:T(1024)S(1)}, s32[4096]{0:T(1024)}, u32[]{:S(2)}) copy-start(s32[4096]{0:T(1024)} %param.12) | copy-start | bytes 49156
  0.6 27.1 %copy-start.3 = (s32[4096]{0:T(1024)S(1)}, s32[4096]{0:T(1024)}, u32[]{:S(2)}) copy-start(s32[4096]{0:T(1024)} %param.13) | copy-start | bytes 49156
  0.7 27.1 %copy-start.4 = (f32[4096]{0:T(1024)S(1)}, f32[4096]{0:T(1024)}, u32[]{:S(2)}) copy-start(f32[4096]{0:T(1024)} %param.14) | copy-start | bytes 49156
  0.7 27.1 %copy-start.5 = (f32[4096]{0:T(1024)S(1)}, f32[4096]{0:T(1024)}, u32[]{:S(2)}) copy-start(f32[4096]{0:T(1024)} %param.15) | copy-start | bytes 49156
  0.7 27.1 %copy-start.6 = (f32[4096]{0:T(1024)S(1)}, f32[4096]{0:T(1024)}, u32[]{:S(2)}) copy-start(f32[4096]{0:T(1024)} %param.16) | copy-start | bytes 49156
  0.7 27.1 %copy-start.7 = (s32[4096]{0:T(1024)S(1)}, s32[4096]{0:T(1024)}, u32[]{:S(2)}) copy-start(s32[4096]{0:T(1024)} %param.17) | copy-start | bytes 49156
  28.6 0.7 %copy-start.1 = (f32[64,512]{1,0:T(8,128)}, f32[64,512]{1,0:T(8,128)S(1)}, u32[]{:S(2)}) copy-start(f32[64,512]{1,0:T(8,128)S(1)} %get-tuple-element.183) | copy-start | bytes 393220
